TPU v7x, 16 devices: a whole 2x2x2 slice. The times are simulated.
16 devices in a mesh: rep: 1, dp: 16 (over x, y, z, core).
Axes of the slice: x: 2, y: 2, z: 2, core: 2. Of those that a mesh axis runs over, the one named last changes fastest.
Arguments:
- x: bfloat16 [16, 2048, 1024], P(('rep', 'dp'))
- dy: bfloat16 [16, 2048, 1024], P(('rep', 'dp'))
- w_gate: bfloat16 [2, 1024, 6144], replicated
- w_up: bfloat16 [2, 1024, 6144], replicated
- w_down: bfloat16 [2, 6144, 1024], replicated
- m_w_gate: float32 [2, 1024, 6144], P(None, 'dp')
- m_w_up: float32 [2, 1024, 6144], P(None, 'dp')
- m_w_down: float32 [2, 6144, 1024], P(None, 'dp')
- v_w_gate: float32 [2, 1024, 6144], P(None, 'dp')
- v_w_up: float32 [2, 1024, 6144], P(None, 'dp')
- v_w_down: float32 [2, 6144, 1024], P(None, 'dp')
Outputs:
- output 1: bfloat16 [2, 1024, 6144], P('rep')
- output 2: bfloat16 [2, 1024, 6144], P('rep')
- output 3: bfloat16 [2, 6144, 1024], P('rep')
- output 4: float32 [2, 1024, 6144], P('rep', 'dp')
- output 5: float32 [2, 1024, 6144], P('rep', 'dp')
- output 6: float32 [2, 6144, 1024], P('rep', 'dp')
- output 7: float32 [2, 1024, 6144], P('rep', 'dp')
- output 8: float32 [2, 1024, 6144], P('rep', 'dp')
- output 9: float32 [2, 6144, 1024], P('rep', 'dp')
All inputs are finite; a program needn't handle non-finite values.
Results may differ from a plain program's by a relative error of at most 0.022.
Values are sent between devices in bfloat16 or wider.
A program may use at most 2 GiB of HBM per device.

v0:
```python
import jax
import jax.numpy as jnp
from jax import lax

NAMES = ("w_gate", "w_up", "w_down")


def matmul(a, w):
    return jnp.dot(a, w, preferred_element_type=jnp.float32).astype(jnp.bfloat16)


def normed(h):
    wide = h.astype(jnp.float32)
    scale = lax.rsqrt(jnp.mean(wide**2, -1, keepdims=True) + 1e-6)
    return (wide * scale).astype(jnp.bfloat16)


def layer(h, w):
    a = normed(h)
    gate = jnp.dot(a, w["w_gate"], preferred_element_type=jnp.float32)
    up = jnp.dot(a, w["w_up"], preferred_element_type=jnp.float32)
    return h + matmul((jax.nn.silu(gate) * up).astype(jnp.bfloat16), w["w_down"])


def adamw(w, m, v, g):
    m = 0.9 * m + 0.1 * g
    v = 0.95 * v + 0.05 * g * g
    step = m * lax.rsqrt(v + 1e-8) + 0.1 * w
    return (w - 0.02 * step).astype(jnp.bfloat16), m, v


def clipped(gradients, sum_of_squares, count):
    factor = jnp.minimum(1.0, 0.5 * lax.rsqrt(sum_of_squares / count + 1e-30))
    return [g * factor for g in gradients]


def stack(weights, h):
    for number in range(weights["w_gate"].shape[0]):
        h = layer(h, {name: w[number] for name, w in weights.items()})
    return h


def solution(mesh):
    groups = mesh.shape["rep"]

    def step(x, dy, *arrays):
        weights, m, v = (arrays[i : i + 3] for i in (0, 3, 6))
        x, dy = (t.reshape(groups, -1, *t.shape[1:]) for t in (x, dy))

        def of_a_group(x, dy):
            _, back = jax.vjp(lambda w: stack(w, x), dict(zip(NAMES, weights, strict=True)))
            by_weights = back(dy)[0]
            gradients = [by_weights[name].astype(jnp.float32) for name in NAMES]
            gradients = clipped(gradients, sum(jnp.sum(g * g) for g in gradients), sum(g.size for g in gradients))
            new = [adamw(w.astype(jnp.float32), m, v, g) for w, m, v, g in zip(weights, m, v, gradients, strict=True)]
            return tuple(one[which] for which in range(3) for one in new)

        return tuple(t.reshape(-1, *t.shape[2:]) for t in jax.vmap(of_a_group)(x, dy))

    return step
```

profile of v0, /device:TPU:0, one launch (start us, length us, event | category | flops | bytes accessed | tf_op | source)
XLA Modules:
  0.0 3039.8 jit_solution(11119781800045594313)
XLA Ops:
  20.4 34.2 %fusion.170 = f32[2048,6144]{1,0:T(8,128)} fusion(bf16[2,1024,6144]{2,1,0:T(8,128)(2,1)} %param.12, bf16[1,2048,1024]{1,2,0:T(8,128)(2,1)S(1)} %fusion.183), kind=kOutput, calls=%fused_computation.214 | convolution fusion | flops 25769803776 | bytes 67108864 | tf_op jit(solution)/vmap(jvp())/dot_general | solution.py:20
  54.6 56.1 %fusion.154 = (bf16[1,2048,6144]{2,1,0:T(8,128)(2,1)}, f32[2048,6144]{1,0:T(8,128)}) fusion(f32[2048,6144]{1,0:T(8,128)} %fusion.170, bf16[2,1024,6144]{2,1,0:T(8,128)(2,1)} %param.17, bf16[1,2048,1024]{1,2,0:T(8,128)(2,1)} %copy-done), kind=kOutput, calls=%fused_computation.189 | convolution fusion | flops 25845301248 | bytes 142606336 | tf_op jit(solution)/vmap(jvp())/dot_general | solution.py:21
  110.7 46.6 %fusion.186 = (f32[2048]{0:T(1024)S(1)}, bf16[1,2048,1024]{1,2,0:T(8,128)(2,1)}) fusion(bf16[1,2048,1024]{1,2,0:T(8,128)(2,1)} %copy.1, bf16[2,6144,1024]{2,1,0:T(8,128)(2,1)} %param.15, bf16[1,2048,6144]{2,1,0:T(8,128)(2,1)} %get-tuple-element.263), kind=kOutput, calls=%fused_computation.233 | convolution fusion | flops 25780287488 | bytes 46145536 | tf_op jit(solution)/vmap(jvp())/dot_general | solution.py:9
  163.4 34.5 %fusion.160 = f32[2048,6144]{1,0:T(8,128)} fusion(bf16[2,1024,6144]{2,1,0:T(8,128)(2,1)} %param.12, bf16[1,2048,1024]{1,2,0:T(8,128)(2,1)S(1)} %fusion.187), kind=kOutput, calls=%fused_computation.204 | convolution fusion | flops 25769803776 | bytes 67108864 | tf_op jit(solution)/vmap(jvp())/dot_general | solution.py:20
  197.9 56.1 %fusion.153 = (bf16[1,2048,6144]{2,1,0:T(8,128)(2,1)}, f32[2048,6144]{1,0:T(8,128)}) fusion(f32[2048,6144]{1,0:T(8,128)} %fusion.160, bf16[2,1024,6144]{2,1,0:T(8,128)(2,1)} %param.17, bf16[1,2048,1024]{1,2,0:T(8,128)(2,1)} %copy-done.1), kind=kOutput, calls=%fused_computation.187 | convolution fusion | flops 25845301248 | bytes 142606336 | tf_op jit(solution)/vmap(jvp())/dot_general | solution.py:21
  254.0 32.7 %copy.3 = bf16[1,2048,6144]{1,2,0:T(8,128)(2,1)} copy(bf16[1,2048,6144]{2,1,0:T(8,128)(2,1)} %get-tuple-element.269) | data formatting | bytes 50331648
  286.7 325.2 %while.16 = (bf16[1,2048,6144]{1,2,0:T(8,128)(2,1)}, bf16[1,2048,1024]{2,1,0:T(8,128)(2,1)}, f32[384,1024]{1,0:T(8,128)S(1)}, f32[384,1024]{1,0:T(8,128)}, u32[]...) while((bf16[1,2048,6144]{1,2,0:T(8,128)(2,1)}, ...), condition=%wide.windowed_dot_general_cond_rs.4.clone, body=%wide.windowed_dot_general_body_rs.4.clone.sunk | while | flops 6457393152 | bytes 115343960 | solution.py:9
  315.1 32.4 %collective-permute-start.18 = (f32[384,1024]{1,0:T(8,128)}, f32[384,1024]{1,0:T(8,128)S(1)}, u32[]{:S(2)}, u32[]{:S(2)}) collective-permute-start(f32[384,1024]{1,0:T(8,128)} %get-tuple-element.492), channel_id=31, source_target_pairs={{0,1},{1,2},{2,3},{3,4},{4,5},{5,6},{6,7},{7,8},{8,9},{9,10},{10,1... | collective-permute-start | bytes 4718600 | tf_op jit(solution)/vmap(transpose(jvp()))/dot_general | solution.py:9
  410.1 17.5 collective-permute-start.18
  451.5 17.6 collective-permute-start.16
  491.6 17.5 collective-permute-start.18
  533.0 17.8 collective-permute-start.16
  573.3 17.5 collective-permute-start.18
  611.9 17.5 collective-permute-start.28
  635.9 32.6 %copy.5 = bf16[1,2048,6144]{1,2,0:T(8,128)(2,1)} copy(bf16[1,2048,6144]{2,1,0:T(8,128)(2,1)} %get-tuple-element.263) | data formatting | bytes 50331648
  668.4 66.6 %convert_multiply_fusion.2 = (bf16[1,2048,6144]{2,1,0:T(8,128)(2,1)}, bf16[1,2048,6144]{2,1,0:T(8,128)(2,1)}) fusion(f32[2048,6144]{1,0:T(8,128)} %fusion.160, f32[2048,6144]{1,0:T(8,128)} %get-tuple-element.270, bf16[2,6144,1024]{2,1,0:T(8,128)(2,1)} %param.15, bf16[1,2048,1024]{2,1,0:T(8,128)(2,1)} %get-tuple-element.744), kind=kOutput, calls=%fused_computation.170 | convolution fusion | flops 25971130368 | bytes 167772160 | tf_op jit(solution)/vmap(transpose(jvp()))/dot_general | solution.py:9
  735.1 34.1 %fusion.146 = bf16[2048,1024]{0,1:T(8,128)(2,1)} fusion(bf16[1,2048,6144]{2,1,0:T(8,128)(2,1)} %get-tuple-element.541, bf16[2,1024,6144]{2,1,0:T(8,128)(2,1)} %param.12), kind=kOutput, calls=%fused_computation.176 | convolution fusion | flops 25769803776 | bytes 41943040 | tf_op jit(solution)/vmap(transpose(jvp()))/dot_general | solution.py:20
  769.2 36.1 %fusion.188 = (f32[2048]{0:T(1024)S(1)}, bf16[2048,1024]{0,1:T(8,128)(2,1)}) fusion(bf16[1,2048,1024]{1,2,0:T(8,128)(2,1)} %get-tuple-element.266, bf16[2048,1024]{0,1:T(8,128)(2,1)} %fusion.146, bf16[2,1024,6144]{2,1,0:T(8,128)(2,1)} %param.17, bf16[1,2048,6144]{2,1,0:T(8,128)(2,1)} %get-tuple-element.613), kind=kOutput, calls=%fused_computation.235 | convolution fusion | flops 25780287488 | bytes 50339840 | tf_op jit(solution)/vmap(transpose(jvp()))/dot_general | solution.py:21
  819.5 323.4 %while.17 = (bf16[1,2048,1024]{2,1,0:T(8,128)(2,1)}, bf16[1,2048,6144]{1,2,0:T(8,128)(2,1)}, f32[1024,384]{0,1:T(8,128)S(1)}, f32[1024,384]{0,1:T(8,128)}, u32[]...) while((bf16[1,2048,1024]{2,1,0:T(8,128)(2,1)}, ...), condition=%wide.windowed_dot_general_cond_rs.5.clone, body=%wide.windowed_dot_general_body_rs.5.clone.sunk | while | flops 6457393152 | bytes 115343960 | solution.py:9
  846.8 32.4 %collective-permute-start.22 = (f32[1024,384]{0,1:T(8,128)}, f32[1024,384]{0,1:T(8,128)S(1)}, u32[]{:S(2)}, u32[]{:S(2)}) collective-permute-start(f32[1024,384]{0,1:T(8,128)} %get-tuple-element.501), channel_id=37, source_target_pairs={{0,1},{1,2},{2,3},{3,4},{4,5},{5,6},{6,7},{7,8},{8,9},{9,10},{10,1... | collective-permute-start | bytes 4718600 | tf_op jit(solution)/vmap(transpose(jvp()))/dot_general | solution.py:9
  982.4 17.5 collective-permute-start.20
  1022.3 17.5 collective-permute-start.22
  1063.7 17.9 collective-permute-start.20
  1104.0 17.5 collective-permute-start.22
  1142.9 17.5 collective-permute-start.29
  1160.4 323.5 %while.14 = (bf16[1,2048,6144]{2,1,0:T(8,128)(2,1)}, bf16[1,2048,1024]{1,2,0:T(8,128)(2,1)}, f32[6144,64]{0,1:T(8,128)S(1)}, f32[6144,64]{0,1:T(8,128)}, u32[]{:...) while((bf16[1,2048,6144]{2,1,0:T(8,128)(2,1)}, ...), condition=%wide.windowed_dot_general_cond_rs.2.clone, body=%wide.windowed_dot_general_body_rs.2.clone.sunk | while | flops 6446907392 | bytes 121635448 | solution.py:21
  1186.3 33.5 %collective-permute-start.10 = (f32[6144,64]{0,1:T(8,128)}, f32[6144,64]{0,1:T(8,128)S(1)}, u32[]{:S(2)}, u32[]{:S(2)}) collective-permute-start(f32[6144,64]{0,1:T(8,128)} %get-tuple-element.474), channel_id=18, source_target_pairs={{0,1},{1,2},{2,3},{3,4},{4,5},{5,6},{6,7},{7,8},{8,9},{9,10},{10,1... | collective-permute-start | bytes 4718600 | tf_op jit(solution)/vmap(transpose(jvp()))/dot_general | solution.py:21
  1243.9 17.4 collective-permute-start.8
  1323.6 19.0 collective-permute-start.8
  1363.7 17.5 collective-permute-start.10
  1405.2 19.0 collective-permute-start.8
  1483.9 19.0 collective-permute-start.26
  1502.9 64.7 %convert_multiply_fusion = (bf16[1,2048,6144]{2,1,0:T(8,128)(2,1)}, bf16[1,2048,6144]{2,1,0:T(8,128)(2,1)}) fusion(f32[2048,6144]{1,0:T(8,128)} %fusion.170, f32[2048,6144]{1,0:T(8,128)} %get-tuple-element.264, bf16[2,6144,1024]{2,1,0:T(8,128)(2,1)} %param.15, bf16[1,2048,1024]{1,2,0:T(8,128)(2,1)} %fusion.189), kind=kOutput, calls=%fused_computation.168 | convolution fusion | flops 25971130368 | bytes 167772160 | tf_op jit(solution)/vmap(transpose(jvp()))/dot_general | solution.py:9
  1567.6 324.5 %while.15 = (bf16[1,2048,6144]{2,1,0:T(8,128)(2,1)}, bf16[1,2048,1024]{1,2,0:T(8,128)(2,1)}, f32[6144,64]{0,1:T(8,128)S(1)}, f32[6144,64]{0,1:T(8,128)}, u32[]{:...) while((bf16[1,2048,6144]{2,1,0:T(8,128)(2,1)}, ...), condition=%wide.windowed_dot_general_cond_rs.3.clone, body=%wide.windowed_dot_general_body_rs.3.clone.sunk | while | flops 6446907392 | bytes 115343960 | solution.py:21
  1595.3 32.4 %collective-permute-start.14 = (f32[6144,64]{0,1:T(8,128)}, f32[6144,64]{0,1:T(8,128)}, u32[]{:S(2)}, u32[]{:S(2)}) collective-permute-start(f32[6144,64]{0,1:T(8,128)} %get-tuple-element.483), channel_id=24, source_target_pairs={{0,1},{1,2},{2,3},{3,4},{4,5},{5,6},{6,7},{7,8},{8,9},{9,10},{10,1... | collective-permute-start | bytes 4718600 | tf_op jit(solution)/vmap(transpose(jvp()))/dot_general | solution.py:21
  1731.4 17.5 collective-permute-start.12
  1771.5 17.5 collective-permute-start.14
  1813.1 17.5 collective-permute-start.12
  1853.3 17.5 collective-permute-start.14
  1893.3 325.8 %while.12 = (bf16[1,2048,6144]{2,1,0:T(8,128)(2,1)}, bf16[1,2048,1024]{1,2,0:T(8,128)(2,1)}, f32[6144,64]{0,1:T(8,128)S(1)}, f32[6144,64]{0,1:T(8,128)}, u32[]{:...) while((bf16[1,2048,6144]{2,1,0:T(8,128)(2,1)}, ...), condition=%wide.windowed_dot_general_cond_rs.clone, body=%wide.windowed_dot_general_body_rs.clone.sunk | while | flops 6446907392 | bytes 115343960 | solution.py:20
  1894.6 17.5 collective-permute-start
  1934.7 17.4 collective-permute-start.2
  1976.2 17.9 collective-permute-start
  2016.8 17.4 collective-permute-start.2
  2058.3 17.5 collective-permute-start
  2098.5 17.4 collective-permute-start.2
  2140.0 17.5 collective-permute-start
  2180.3 17.4 collective-permute-start.2
  2219.1 326.1 %while.13 = (bf16[1,2048,6144]{2,1,0:T(8,128)(2,1)}, bf16[1,2048,1024]{1,2,0:T(8,128)(2,1)}, f32[6144,64]{0,1:T(8,128)S(1)}, f32[6144,64]{0,1:T(8,128)}, u32[]{:...) while((bf16[1,2048,6144]{2,1,0:T(8,128)(2,1)}, ...), condition=%wide.windowed_dot_general_cond_rs.1.clone, body=%wide.windowed_dot_general_body_rs.1.clone.sunk | while | flops 6446907392 | bytes 115343960 | solution.py:20
  2220.6 17.5 collective-permute-start.4
  2260.8 17.5 collective-permute-start.6
  2302.3 17.9 collective-permute-start.4
  2342.9 17.5 collective-permute-start.6
  2384.4 17.5 collective-permute-start.4
  2424.5 17.5 collective-permute-start.6
  2466.1 17.5 collective-permute-start.4
  2506.3 17.5 collective-permute-start.6
  2545.2 17.5 collective-permute-start.27
  2605.6 48.2 %all-reduce.10 = f32[]{:T(128)} all-reduce(f32[]{:T(128)S(6)} %add.180), channel_id=13, replica_groups=mesh['rep'=1,'dp'=16] {'dp'}, use_global_device_ids=true, to_apply=%region_3.4.clone | all-reduce | flops 1 | bytes 8 | tf_op jit(solution)/vmap()/reduce_sum | solution.py:54
  2673.7 91.6 %all-gather.14.cloned.1.call-done = bf16[1,2,6144,1024]{3,2,1,0:T(8,128)(2,1)} async-done(((bf16[1,2,384,1024]{3,2,1,0:T(8,128)(2,1)}), bf16[1,2,6144,1024]{3,2,1,0:T(8,128)(2,1)}) %all-gather.14.cloned.1.call-update) | async-done | bytes 25165840 | tf_op jit(solution)/reshape | solution.py:58
  2765.3 106.2 %all-gather.12.cloned.1.call-done = bf16[1,2,1024,6144]{3,2,1,0:T(8,128)(2,1)} async-done(((bf16[1,2,64,6144]{3,2,1,0:T(8,128)(2,1)}), bf16[1,2,1024,6144]{3,2,1,0:T(8,128)(2,1)}) %all-gather.12.cloned.1.call-update) | async-done | bytes 25165840 | tf_op jit(solution)/reshape | solution.py:58
  2871.4 106.2 %all-gather.10.cloned.1.call-done = bf16[1,2,1024,6144]{3,2,1,0:T(8,128)(2,1)} async-done(((bf16[1,2,64,6144]{3,2,1,0:T(8,128)(2,1)}), bf16[1,2,1024,6144]{3,2,1,0:T(8,128)(2,1)}) %all-gather.10.cloned.1.call-update) | async-done | bytes 25165840 | tf_op jit(solution)/reshape | solution.py:58
  2977.6 23.1 copy.63
  3000.8 23.1 copy.64
  (430 shorter events, 1345.1 us)
Async XLA Ops:
  7.2 2758.1 %all-gather.14.cloned.1.call-start = ((), (), s32[]{:S(2)}) async-start(), calls=%async_computation.2 | async-start | bytes 26738688 | tf_op jit(solution)/reshape | solution.py:58
  288.1 22.8 collective-permute-start.16
  290.1 21.9 collective-permute-start.17
  315.1 38.5 %collective-permute-start.18 = (f32[384,1024]{1,0:T(8,128)}, f32[384,1024]{1,0:T(8,128)S(1)}, u32[]{:S(2)}, u32[]{:S(2)}) collective-permute-start(f32[384,1024]{1,0:T(8,128)} %get-tuple-element.492), channel_id=31, source_target_pairs={{0,1},{1,2},{2,3},{3,4},{4,5},{5,6},{6,7},{7,8},{8,9},{9,10},{10,1... | collective-permute-start | bytes 4718600 | tf_op jit(solution)/vmap(transpose(jvp()))/dot_general | solution.py:9
  371.5 23.6 collective-permute-start.16
  410.1 23.6 collective-permute-start.18
  451.5 25.0 collective-permute-start.16
  491.6 23.6 collective-permute-start.18
  533.0 25.2 collective-permute-start.16
  573.3 23.6 collective-permute-start.18
  611.9 1953.3 %collective-permute-start.28 = (f32[384,1024]{1,0:T(8,128)}, f32[384,1024]{1,0:T(8,128)}, u32[]{:S(2)}, u32[]{:S(2)}) collective-permute-start(f32[384,1024]{1,0:T(8,128)} %get-tuple-element.45), channel_id=32, source_target_pairs={{0,1},{1,2},{2,3},{3,4},{4,5},{5,6},{6,7},{7,8},{8,9},{9,10},{10,1... | collective-permute-start | bytes 4718600 | tf_op jit(solution)/vmap(transpose(jvp()))/dot_general | solution.py:9
  820.8 21.7 collective-permute-start.20
  824.6 19.0 collective-permute-start.21
  846.8 38.5 %collective-permute-start.22 = (f32[1024,384]{0,1:T(8,128)}, f32[1024,384]{0,1:T(8,128)S(1)}, u32[]{:S(2)}, u32[]{:S(2)}) collective-permute-start(f32[1024,384]{0,1:T(8,128)} %get-tuple-element.501), channel_id=37, source_target_pairs={{0,1},{1,2},{2,3},{3,4},{4,5},{5,6},{6,7},{7,8},{8,9},{9,10},{10,1... | collective-permute-start | bytes 4718600 | tf_op jit(solution)/vmap(transpose(jvp()))/dot_general | solution.py:9
  903.2 23.6 collective-permute-start.20
  941.8 22.7 collective-permute-start.22
  982.4 24.9 collective-permute-start.20
  1022.3 23.6 collective-permute-start.22
  1063.7 25.3 collective-permute-start.20
  1104.0 23.6 collective-permute-start.22
  1142.9 1424.5 %collective-permute-start.29 = (f32[1024,384]{0,1:T(8,128)}, f32[1024,384]{0,1:T(8,128)}, u32[]{:S(2)}, u32[]{:S(2)}) collective-permute-start(f32[1024,384]{0,1:T(8,128)} %get-tuple-element.47), channel_id=38, source_target_pairs={{0,1},{1,2},{2,3},{3,4},{4,5},{5,6},{6,7},{7,8},{8,9},{9,10},{10,1... | collective-permute-start | bytes 4718600 | tf_op jit(solution)/vmap(transpose(jvp()))/dot_general | solution.py:9
  1161.7 21.7 collective-permute-start.8
  1164.3 19.1 collective-permute-start.9
  1186.3 43.6 %collective-permute-start.10 = (f32[6144,64]{0,1:T(8,128)}, f32[6144,64]{0,1:T(8,128)S(1)}, u32[]{:S(2)}, u32[]{:S(2)}) collective-permute-start(f32[6144,64]{0,1:T(8,128)} %get-tuple-element.474), channel_id=18, source_target_pairs={{0,1},{1,2},{2,3},{3,4},{4,5},{5,6},{6,7},{7,8},{8,9},{9,10},{10,1... | collective-permute-start | bytes 4718600 | tf_op jit(solution)/vmap(transpose(jvp()))/dot_general | solution.py:21
  1243.9 27.7 collective-permute-start.8
  1261.3 18.0 collective-permute-start.9
  1282.3 27.3 collective-permute-start.10
  1323.6 29.3 collective-permute-start.8
  1342.7 18.0 collective-permute-start.9
  1363.7 27.7 collective-permute-start.10
  1405.2 29.3 collective-permute-start.8
  1424.3 18.0 collective-permute-start.9
  1445.3 27.3 collective-permute-start.10
  1483.9 1085.6 %collective-permute-start.26 = (f32[6144,64]{0,1:T(8,128)}, f32[6144,64]{0,1:T(8,128)}, u32[]{:S(2)}, u32[]{:S(2)}) collective-permute-start(f32[6144,64]{0,1:T(8,128)} %get-tuple-element.41), channel_id=19, source_target_pairs={{0,1},{1,2},{2,3},{3,4},{4,5},{5,6},{6,7},{7,8},{8,9},{9,10},{10,1... | collective-permute-start | bytes 4718600 | tf_op jit(solution)/vmap(transpose(jvp()))/dot_general | solution.py:21
  1569.1 21.7 collective-permute-start.12
  1572.9 19.0 collective-permute-start.13
  1595.3 42.5 %collective-permute-start.14 = (f32[6144,64]{0,1:T(8,128)}, f32[6144,64]{0,1:T(8,128)}, u32[]{:S(2)}, u32[]{:S(2)}) collective-permute-start(f32[6144,64]{0,1:T(8,128)} %get-tuple-element.483), channel_id=24, source_target_pairs={{0,1},{1,2},{2,3},{3,4},{4,5},{5,6},{6,7},{7,8},{8,9},{9,10},{10,1... | collective-permute-start | bytes 4718600 | tf_op jit(solution)/vmap(transpose(jvp()))/dot_general | solution.py:21
  1651.8 27.6 collective-permute-start.12
  1690.7 26.7 collective-permute-start.14
  1731.4 28.9 collective-permute-start.12
  1771.5 27.6 collective-permute-start.14
  1813.1 28.9 collective-permute-start.12
  1853.3 27.6 collective-permute-start.14
  1894.6 28.9 collective-permute-start
  1934.7 27.6 collective-permute-start.2
  1976.2 29.3 collective-permute-start
  2016.8 27.6 collective-permute-start.2
  2058.3 28.9 collective-permute-start
  2098.5 27.6 collective-permute-start.2
  2140.0 29.0 collective-permute-start
  2180.3 27.6 collective-permute-start.2
  2220.6 28.9 collective-permute-start.4
  2260.8 27.6 collective-permute-start.6
  2302.3 29.3 collective-permute-start.4
  2342.9 27.6 collective-permute-start.6
  2384.4 28.9 collective-permute-start.4
  2424.5 27.6 collective-permute-start.6
  2466.1 28.9 collective-permute-start.4
  2506.3 27.6 collective-permute-start.6
  2545.2 26.2 collective-permute-start.27
  2562.7 21.6 collective-permute-start.24
  2565.2 36.0 %collective-permute-start.25 = (f32[6144,64]{0,1:T(8,128)}, f32[6144,64]{0,1:T(8,128)S(1)}, u32[]{:S(2)}, u32[]{:S(2)}) collective-permute-start(f32[6144,64]{0,1:T(8,128)} %get-tuple-element.39), channel_id=12, source_target_pairs={{0,1},{1,2},{2,3},{3,4},{4,5},{5,6},{6,7},{7,8},{8,9},{9,10},{10,1... | collective-permute-start | bytes 4718600 | tf_op jit(solution)/vmap(transpose(jvp()))/dot_general | solution.py:20
  2661.0 210.4 %all-gather.12.cloned.1.call-start = ((), (), s32[]{:S(2)}) async-start(), calls=%async_computation.1 | async-start | bytes 26738688 | tf_op jit(solution)/reshape | solution.py:58
  2667.4 310.2 %all-gather.10.cloned.1.call-start = ((), (), s32[]{:S(2)}) async-start(), calls=%async_computation | async-start | bytes 26738688 | tf_op jit(solution)/reshape | solution.py:58
  (81 other events, 2065.0 us)
Sparse Core Ops, SparseCore 0:
  2661.1 104.0 all-gather.13
  2768.1 103.3 all-gather.11
  2874.3 103.3 all-gather.9
where the time goes:
time: 3050 us; the launch traced here: 3040 us
  starting transfers between devices  918 us (30%)
  matrix products  851 us (28%)
  waiting for transfers between devices  764 us (25%)
  other arithmetic  289 us (9%)
  local copies, waits for them, and re-layouts  151 us (5%)
  blocking collectives  48.2 us (2%)
    dot_general x34, starting transfers between devices, layer(): up = jnp.dot(a, w['w_up'], preferred_element_type=jnp.float32)  320 us
    dot_general x34, starting transfers between devices, matmul(): jnp.dot(a, w, preferred_element_type=jnp.float32).astype(jnp.bfloat16)  315 us
    dot_general x19, matrix products, layer(): up = jnp.dot(a, w['w_up'], preferred_element_type=jnp.float32)  310 us
    reshape x3, waiting for transfers between devices, step(): t.reshape(-1, *t.shape[2:])  304 us
    dot_general x34, starting transfers between devices, layer(): gate = jnp.dot(a, w['w_gate'], preferred_element_type=jnp.float32)  283 us
    dot_general x19, matrix products, matmul(): jnp.dot(a, w, preferred_element_type=jnp.float32).astype(jnp.bfloat16)  276 us
    dot_general x19, matrix products, layer(): gate = jnp.dot(a, w['w_gate'], preferred_element_type=jnp.float32)  265 us
    dot_general x34, waiting for transfers between devices, matmul(): jnp.dot(a, w, preferred_element_type=jnp.float32).astype(jnp.bfloat16)  189 us
  transfers between devices with their start and end apart: 105, of which 56 were waited for; matrix products, arithmetic and copies ran while one was open for 30% of the time, Pallas kernels for 0%

commit v1 on v0

v1 whole, which is shorter than its diff:
```python
import functools

import jax
import jax.numpy as jnp
from jax import lax
from jax.experimental import pallas as pl
from jax.experimental.pallas import tpu as pltpu
from jax.sharding import PartitionSpec as P

F32, BF16 = jnp.float32, jnp.bfloat16
EPS = 1e-6
MIB = 1 << 20


def dot(a, b, ca, cb):
    return lax.dot_general(a, b, (((ca,), (cb,)), ((), ())), preferred_element_type=F32)


def call(kernel, flops, nbytes, vmem, **kw):
    return pl.pallas_call(
        kernel,
        compiler_params=pltpu.CompilerParams(vmem_limit_bytes=vmem * MIB, dimension_semantics=("arbitrary",)),
        cost_estimate=pl.CostEstimate(flops=flops, bytes_accessed=nbytes, transcendentals=0),
        **kw,
    )


def whole(*shape):
    return pl.BlockSpec(shape, lambda i: (0,) * len(shape), pipeline_mode=pl.Buffered(1))


def normed(h):
    wide = h.astype(F32)
    return (wide * lax.rsqrt(jnp.mean(wide * wide, -1, keepdims=True) + EPS)).astype(BF16)


def gate_up_kernel(a_ref, wg_ref, wu_ref, gate_ref, up_ref, act_ref):
    gate = dot(a_ref[...], wg_ref[0], 1, 0)
    up = dot(a_ref[...], wu_ref[0], 1, 0)
    gate_ref[...] = gate
    up_ref[...] = up
    act_ref[...] = (gate * jax.nn.sigmoid(gate) * up).astype(BF16)


def gate_up(a, wg, wu, bn=256):
    t, d = a.shape
    f = wg.shape[2]
    w = pl.BlockSpec((1, d, bn), lambda j: (0, 0, j))
    o = pl.BlockSpec((t, bn), lambda j: (0, j))
    return call(
        gate_up_kernel, 4 * t * d * f, 10 * t * f + 4 * d * f, 56,
        grid=(f // bn,),
        in_specs=[whole(t, d), w, w],
        out_specs=[o, o, o],
        out_shape=[jax.ShapeDtypeStruct((t, f), F32)] * 2 + [jax.ShapeDtypeStruct((t, f), BF16)],
        name="gate_up",
    )(a, wg, wu)


def down_kernel(act_ref, wd_ref, x_ref, h_ref, a_ref):
    h = x_ref[...] + dot(act_ref[...], wd_ref[0], 1, 0).astype(BF16)
    h_ref[...] = h
    a_ref[...] = normed(h)


def down(act, wd, x, bm=512):
    t, f = act.shape
    d = x.shape[1]
    r = pl.BlockSpec((bm, d), lambda i: (i, 0))
    return call(
        down_kernel, 2 * t * d * f, 2 * (t * f + d * f), 60,
        grid=(t // bm,),
        in_specs=[pl.BlockSpec((bm, f), lambda i: (i, 0)), whole(1, f, d), r],
        out_specs=[r, r],
        out_shape=[jax.ShapeDtypeStruct((t, d), BF16)] * 2,
        name="down",
    )(act, wd, x)


def back_through_product(gate, up, dact):
    dact = dact.astype(BF16).astype(F32)
    sig = jax.nn.sigmoid(gate)
    silu = gate * sig
    dgate = dact * up * (sig + silu * (1.0 - sig))
    return (silu * up).astype(BF16), dgate.astype(BF16), (dact * silu).astype(BF16)


def put_terms(p_ref, stage_g, stage_u, stage_d, sems, j, steps, act, dgate, dup, a, dh, bn):
    n, blocks = p_ref.shape[:2]
    blocks = blocks // 3
    slot = lax.rem(j, 2)
    per = p_ref.shape[3] // bn

    def copies(slot, j):
        out = []
        for which, stage in enumerate((stage_g, stage_u)):
            part = p_ref.at[:, blocks * (1 + which) + lax.div(j, per), :, pl.ds(pl.multiple_of(lax.rem(j, per) * bn, bn), bn)]
            out.append(pltpu.make_async_copy(stage.at[slot], part, sems.at[slot, which]))
        first = j * (bn // 64)
        for i in range(bn // 64):
            to = p_ref.at[lax.div(first + i, blocks), lax.rem(first + i, blocks)]
            out.append(pltpu.make_async_copy(stage_d.at[slot, i], to, sems.at[slot, 2 + i]))
        return out

    @pl.when(j >= 2)
    def _():
        for c in copies(slot, j - 2):
            c.wait()

    for stage, cot in ((stage_g, dgate), (stage_u, dup)):
        stage[slot] = dot(a[...], cot, 0, 0).astype(BF16).reshape(stage.shape[1:])
    stage_d[slot] = dot(act, dh[...], 0, 0).astype(BF16).reshape(stage_d.shape[1:])
    for c in copies(slot, j):
        c.start()

    @pl.when(j == steps - 1)
    def _():
        for c in copies(1 - slot, j - 1) + copies(slot, j):
            c.wait()


def term_scratch(n, d, bn):
    return [
        pltpu.VMEM((2, n, d // n, bn), BF16),
        pltpu.VMEM((2, n, d // n, bn), BF16),
        pltpu.VMEM((2, bn // 64, 64, d), BF16),
        pltpu.SemaphoreType.DMA((2, 2 + bn // 64)),
    ]


def last_layer_kernel(steps, bn, a_ref, dy_ref, wg_ref, wu_ref, wd_ref, dgate_ref, dup_ref, p_ref, *scratch):
    gate = dot(a_ref[...], wg_ref[0], 1, 0)
    up = dot(a_ref[...], wu_ref[0], 1, 0)
    dact = dot(dy_ref[...], wd_ref[0], 1, 1)
    act, dgate, dup = back_through_product(gate, up, dact)
    dgate_ref[...] = dgate
    dup_ref[...] = dup
    put_terms(p_ref, *scratch, pl.program_id(0), steps, act, dgate, dup, a_ref, dy_ref, bn)


def last_layer(a, dy, wg, wu, wd, n, bn=512):
    t, d = a.shape
    f = wg.shape[2]
    last = wg.shape[0] - 1
    steps = f // bn
    w = pl.BlockSpec((1, d, bn), lambda j: (last, 0, j))
    o = pl.BlockSpec((t, bn), lambda j: (0, j))
    return call(
        functools.partial(last_layer_kernel, steps, bn), 12 * t * d * f, 4 * t * f + 12 * d * f, 60,
        grid=(steps,),
        in_specs=[whole(t, d), whole(t, d), w, w, pl.BlockSpec((1, bn, d), lambda j: (last, j, 0))],
        out_specs=[o, o, pl.BlockSpec(memory_space=pl.ANY)],
        out_shape=[jax.ShapeDtypeStruct((t, f), BF16)] * 2 + [jax.ShapeDtypeStruct((n, 3 * f // n // 64, 64, d), BF16)],
        scratch_shapes=term_scratch(n, d, bn),
        name="last_layer",
    )(a, dy, wg, wu, wd)


def to_input_kernel(dgate_ref, dup_ref, wg_ref, wu_ref, h_ref, dy_ref, dh_ref):
    da = dot(dgate_ref[...], wg_ref[0], 1, 1).astype(BF16) + dot(dup_ref[...], wu_ref[0], 1, 1).astype(BF16)
    da = da.astype(F32)
    wide = h_ref[...].astype(F32)
    scale = lax.rsqrt(jnp.mean(wide * wide, -1, keepdims=True) + EPS)
    inner = jnp.mean(da * wide, -1, keepdims=True)
    dwide = da * scale - wide * (scale * scale * scale * inner)
    dh_ref[...] = dy_ref[...] + dwide.astype(BF16)


def to_input(dgate, dup, wg, wu, h, dy, bm=256):
    t, f = dgate.shape
    d = h.shape[1]
    last = wg.shape[0] - 1
    c = pl.BlockSpec((bm, f), lambda i: (i, 0))
    r = pl.BlockSpec((bm, d), lambda i: (i, 0))
    w = pl.BlockSpec((1, d, f), lambda i: (last, 0, 0), pipeline_mode=pl.Buffered(1))
    return call(
        to_input_kernel, 4 * t * d * f, 4 * t * f + 4 * d * f, 60,
        grid=(t // bm,),
        in_specs=[c, c, w, w, r, r],
        out_specs=r,
        out_shape=jax.ShapeDtypeStruct((t, d), BF16),
        name="to_input",
    )(dgate, dup, wg, wu, h, dy)


def first_layer_kernel(steps, bn, gate_ref, up_ref, a_ref, dh_ref, wd_ref, p_ref, *scratch):
    dact = dot(dh_ref[...], wd_ref[0], 1, 1)
    act, dgate, dup = back_through_product(gate_ref[...], up_ref[...], dact)
    put_terms(p_ref, *scratch, pl.program_id(0), steps, act, dgate, dup, a_ref, dh_ref, bn)


def first_layer(gate, up, a, dh, wd, n, bn=512):
    t, d = a.shape
    f = gate.shape[1]
    steps = f // bn
    c = pl.BlockSpec((t, bn), lambda j: (0, j))
    return call(
        functools.partial(first_layer_kernel, steps, bn), 8 * t * d * f, 8 * t * f + 8 * d * f, 60,
        grid=(steps,),
        in_specs=[c, c, whole(t, d), whole(t, d), pl.BlockSpec((1, bn, d), lambda j: (0, j, 0))],
        out_specs=pl.BlockSpec(memory_space=pl.ANY),
        out_shape=jax.ShapeDtypeStruct((n, 3 * f // n // 64, 64, d), BF16),
        scratch_shapes=term_scratch(n, d, bn),
        name="first_layer",
    )(gate, up, a, dh, wd)


ORDERS = ((0, 1, 2), (1, 2, 0), (2, 0, 1))
MESH = pl.DeviceIdType.MESH


def place():
    me = lax.axis_index("dp")
    bits = (lax.rem(me // 8, 2), lax.rem(me // 4, 2), lax.rem(me // 2, 2))
    return me, bits, lax.rem(me, 2)


def neighbour(me, bits, axis):
    step = (8, 4, 2)[axis]
    return {"dp": me + step * (1 - 2 * bits[axis])}


def greet_all(me, n):
    barrier = pltpu.get_barrier_semaphore()

    @pl.loop(1, n)
    def _(i):
        pl.semaphore_signal(barrier, inc=1, device_id={"dp": lax.rem(me + i, n)}, device_id_type=MESH)

    pl.semaphore_wait(barrier, n - 1)


def at(fixed, among):
    return tuple(fixed.get(a, slice(None)) for a in among)


def reduce_kernel(
    n, chunks, p_ref, g1_ref, g_ref, total_ref, own, from_core, from_a, from_b, from_c, square, squares,
    own_sem, core_send, core_recv, a_send, a_recv, b_send, b_recv, c_send, c_recv, sq_send, sq_recv,
):
    me, bits, core = place()
    partner = {"dp": me + 1 - 2 * core}
    slots = own.shape[0]
    greet_all(me, n)

    def own_copy(i, q):
        src = p_ref.at[:, :, :, core, q * chunks + i]
        return pltpu.make_async_copy(src, own.at[lax.rem(i, slots), q], own_sem.at[lax.rem(i, slots), q])

    def core_copy(i, q):
        return pltpu.make_async_remote_copy(
            src_ref=p_ref.at[:, :, :, 1 - core, q * chunks + i], dst_ref=from_core.at[i, q],
            send_sem=core_send.at[i, q], recv_sem=core_recv.at[i, q], device_id=partner, device_id_type=MESH,
        )

    def indices(q):
        one, two, three = ORDERS[q]
        here = {a: bits[a] for a in range(3)}
        there = {a: 1 - bits[a] for a in range(3)}
        rest = tuple(a for a in range(3) if a != one)
        a_full = at({one: there[one]}, (0, 1, 2))
        b_full = at({one: here[one], two: there[two]}, (0, 1, 2))
        b_in_a = at({two: there[two]}, rest)
        c_full = at({one: here[one], two: here[two], three: there[three]}, (0, 1, 2))
        c_in_a = at({two: here[two], three: there[three]}, rest)
        mine = at(here, (0, 1, 2))
        mine_in_a = at({two: here[two], three: here[three]}, rest)
        return a_full, b_full, b_in_a, c_full, c_in_a, (there[three],), mine, mine_in_a, (here[three],)

    def step_copy(i, q, stage):
        a_full, _, b_in_a, _, _, c_in_b, *_ = indices(q)
        src, dst, send, recv = (
            (from_core.at[(i, q) + a_full], from_a.at[i, q], a_send, a_recv),
            (from_a.at[(i, q) + b_in_a], from_b.at[i, q], b_send, b_recv),
            (from_b.at[(i, q) + c_in_b], from_c.at[i, q], c_send, c_recv),
        )[stage]
        return pltpu.make_async_remote_copy(
            src_ref=src, dst_ref=dst, send_sem=send.at[i, q], recv_sem=recv.at[i, q],
            device_id=neighbour(me, bits, ORDERS[q][stage]), device_id_type=MESH,
        )

    def add(parts):
        total = parts[0].astype(F32)
        for part in parts[1:]:
            total = total + part.astype(F32)
        return total

    for i in range(chunks):
        for q in range(3):
            core_copy(i, q).start()
            if i == 0:
                own_copy(i, q).start()
    square[...] = jnp.zeros_like(square)

    @pl.loop(0, g1_ref.shape[0])
    def _(b):
        wide = g1_ref[b].astype(F32)
        square[...] += fold(wide * wide)

    @pl.loop(0, chunks + 3)
    def _(s):
        @pl.when(s < chunks)
        def _():
            for q in range(3):
                own_copy(s, q).wait()
                core_copy(s, q).wait_recv()
                a_full = indices(q)[0]
                o, k = (lax.rem(s, slots), q) + a_full, (s, q) + a_full
                from_core[k] = add([own[o], from_core[k]]).astype(BF16)
                step_copy(s, q, 0).start()

        @pl.when((s >= 1) & (s < chunks + 1))
        def _():
            i = s - 1
            for q in range(3):
                step_copy(i, q, 0).wait_recv()
                _, b_full, b_in_a, *_ = indices(q)
                o, k, ka = (lax.rem(i, slots), q) + b_full, (i, q) + b_full, (i, q) + b_in_a
                from_a[ka] = add([own[o], from_core[k], from_a[ka]]).astype(BF16)
                step_copy(i, q, 1).start()

        @pl.when((s >= 2) & (s < chunks + 2))
        def _():
            i = s - 2
            for q in range(3):
                step_copy(i, q, 1).wait_recv()
                _, _, _, c_full, c_in_a, c_in_b, *_ = indices(q)
                o, k, ka, kb = (lax.rem(i, slots), q) + c_full, (i, q) + c_full, (i, q) + c_in_a, (i, q) + c_in_b
                from_b[kb] = add([own[o], from_core[k], from_a[ka], from_b[kb]]).astype(BF16)
                step_copy(i, q, 2).start()

        @pl.when(s >= 3)
        def _():
            i = s - 3
            for q in range(3):
                step_copy(i, q, 2).wait_recv()
                *_, mine, mine_in_a, mine_in_b = indices(q)
                o, k, ka, kb = (lax.rem(i, slots), q) + mine, (i, q) + mine, (i, q) + mine_in_a, (i, q) + mine_in_b
                g = add([own[o], from_core[k], from_a[ka], from_b[kb], from_c[i, q]]).astype(BF16)
                g_ref[q * chunks + i] = g
                wide = g.astype(F32)
                square[...] += fold(wide * wide)

        @pl.when(s + 1 < chunks)
        def _():
            for q in range(3):
                own_copy(s + 1, q).start()

    squares[me] = square[...]

    def square_copy(i):
        return pltpu.make_async_remote_copy(
            src_ref=square, dst_ref=squares.at[me], send_sem=sq_send.at[i], recv_sem=sq_recv.at[me],
            device_id={"dp": lax.rem(me + i, n)}, device_id_type=MESH,
        )

    def square_arrival(i):
        other = lax.rem(me + i, n)
        return pltpu.make_async_remote_copy(
            src_ref=square, dst_ref=squares.at[other], send_sem=sq_send.at[i], recv_sem=sq_recv.at[other],
            device_id={"dp": other}, device_id_type=MESH,
        )

    @pl.loop(1, n)
    def _(i):
        square_copy(i).start()

    @pl.loop(0, chunks)
    def _(i):
        for q in range(3):
            core_copy(i, q).wait_send()
            for stage in range(3):
                step_copy(i, q, stage).wait_send()

    @pl.loop(1, n)
    def _(i):
        square_copy(i).wait_send()
        square_arrival(i).wait_recv()

    total = squares[0]
    for i in range(1, n):
        total = total + squares[i]
    total_ref[...] = total


def fold(wide):
    rows, columns = wide.shape
    rows8 = wide[:8]
    for r in range(8, rows, 8):
        rows8 = rows8 + wide[r : r + 8]
    total = rows8[:, :128]
    for c in range(128, columns, 128):
        total = total + rows8[:, c : c + 128]
    return total


def reduce_scatter(p, g1):
    n, blocks, rows, d = p.shape
    chunks = blocks // 3
    sem = pltpu.SemaphoreType.DMA
    cells = lambda *lead: pltpu.VMEM(lead + (rows, d), BF16)
    return pl.pallas_call(
        functools.partial(reduce_kernel, n, chunks),
        in_specs=[pl.BlockSpec(memory_space=pl.ANY), pl.BlockSpec(memory_space=pltpu.VMEM)],
        out_specs=[pl.BlockSpec(memory_space=pltpu.VMEM)] * 2,
        out_shape=[jax.ShapeDtypeStruct((blocks, rows, d), BF16), jax.ShapeDtypeStruct((8, 128), F32)],
        scratch_shapes=[
            cells(4, 3, 2, 2, 2), cells(chunks, 3, 2, 2, 2), cells(chunks, 3, 2, 2), cells(chunks, 3, 2), cells(chunks, 3),
            pltpu.VMEM((8, 128), F32), pltpu.VMEM((n, 8, 128), F32), sem((4, 3)),
        ] + [sem((chunks, 3))] * 8 + [sem((n,))] * 2,
        compiler_params=pltpu.CompilerParams(vmem_limit_bytes=62 * MIB, collective_id=0, has_side_effects=True),
        cost_estimate=pl.CostEstimate(flops=200_000_000_000, bytes_accessed=6 * p.size, transcendentals=0),
        name="reduce_scatter",
    )(p.reshape(2, 2, 2, 2, blocks, rows, d), g1)


def adamw(w, m, v, g):
    m = 0.9 * m + 0.1 * g
    v = 0.95 * v + 0.05 * g * g
    step = m * lax.rsqrt(v + 1e-8) + 0.1 * w
    return (w - 0.02 * step).astype(BF16), m, v


def terms(x, dy, wg, wu, wd, n):
    a0 = normed(x)
    gate, up, act = gate_up(a0, wg, wu)
    h1, a1 = down(act, wd, x)
    dgate, dup, p1 = last_layer(a1, dy, wg, wu, wd, n)
    dh = to_input(dgate, dup, wg, wu, h1, dy)
    p0 = first_layer(gate, up, a0, dh, wd, n)
    return p1, p0


def unpacked(g, blocks):
    wide = lambda t: t.transpose(1, 0, 2).reshape(64, -1)
    return wide(g[blocks : 2 * blocks]), wide(g[2 * blocks :]), g[:blocks].reshape(-1, g.shape[-1])


def solution(mesh):
    n = mesh.shape["dp"]

    def step(x, dy, *arrays):
        w, m, v = (arrays[i : i + 3] for i in (0, 3, 6))
        packed = terms(x[0], dy[0], *w, n)
        blocks = packed[0].shape[1] // 3
        g1 = lax.psum_scatter(packed[0], "dp", scatter_dimension=0, tiled=True)[0]
        g0, squares = reduce_scatter(packed[1], g1)
        by_layer = [[g.astype(F32) for g in unpacked(s, blocks)] for s in (g0, g1)]
        count = sum(a.size for a in w)
        square = jnp.sum(squares)
        factor = jnp.minimum(1.0, 0.5 * lax.rsqrt(square / count + 1e-30))
        me = lax.axis_index("dp")
        new = [[], [], []]
        for i in range(3):
            rows = m[i].shape[1]
            each = []
            for layer in range(2):
                own = lax.dynamic_slice(w[i], (layer, me * rows, 0), (1, rows, w[i].shape[2]))[0].astype(F32)
                each.append(adamw(own, m[i][layer], v[i][layer], by_layer[layer][i] * factor))
            gathered = [lax.all_gather(e[0], "dp", axis=0, tiled=True) for e in each]
            new[0].append(jnp.stack(gathered))
            new[1].append(jnp.stack([e[1] for e in each]))
            new[2].append(jnp.stack([e[2] for e in each]))
        return tuple(new[0] + new[1] + new[2])

    rows, all_ = P("dp"), P()
    moment, out_moment = P(None, "dp"), P("rep", "dp")
    return jax.shard_map(
        step,
        mesh=mesh,
        in_specs=(rows, rows) + (all_,) * 3 + (moment,) * 6,
        out_specs=(P("rep"),) * 3 + (out_moment,) * 6,
        check_vma=False,
    )
```

time: 3050 us -> 1090 us (0.36)
  starting transfers between devices: 918 us -> 0.28 us
  matrix products: 851 us -> 0 us
  Pallas kernels: 0 us -> 642 us
  waiting for transfers between devices: 764 us -> 284 us
  other arithmetic: 289 us -> 105 us
  local copies, waits for them, and re-layouts: 151 us -> 39.2 us
  blocking collectives: 48.2 us -> 0 us
    dot_general x102 -> x0, starting transfers between devices: 917 us -> none  [the longest x34 320 us: layer(): up = jnp.dot(a, w['w_up'], preferred_element_type=jnp.float32)]
    dot_general x57 -> x0, matrix products: 851 us -> none  [the longest x19 310 us: layer(): up = jnp.dot(a, w['w_up'], preferred_element_type=jnp.float32)]
    pallas_call x0 -> x6, Pallas kernels: none -> 642 us  [the longest x1 201 us: last_layer(): call(functools.partial(last_layer_kernel, steps, bn), 12 * t * d * f, 4 *...]
    dot_general x102 -> x0, waiting for transfers between devices: 460 us -> none  [the longest x34 189 us: matmul(): jnp.dot(a, w, preferred_element_type=jnp.float32).astype(jnp.bfloat16)]
    reshape x3 -> x0, waiting for transfers between devices: 304 us -> none  [step(): t.reshape(-1, *t.shape[2:])]
    all_gather x0 -> x6, waiting for transfers between devices: none -> 281 us  [step(): gathered = [lax.all_gather(e[0], 'dp', axis=0, tiled=True) for e in each]]
    dot_general x96 -> x0, other arithmetic: 242 us -> none
    unnamed x80 -> x28, local copies, waits for them, and re-layouts: 147 us -> 8.99 us
  transfers between devices with their start and end apart: 105 -> 7, of which waited for: 56 -> 6; matrix products, arithmetic and copies ran while one was open for 30% -> 9% of each run, Pallas kernels for 0% -> 19%
where the time goes in v1:
time: 1090 us
  Pallas kernels  642 us (59%)
  waiting for transfers between devices  284 us (26%)
  other arithmetic  105 us (10%)
  local copies, waits for them, and re-layouts  39.2 us (4%)
  between operations  15.4 us (1%)
    all_gather x6, waiting for transfers between devices, step(): gathered = [lax.all_gather(e[0], 'dp', axis=0, tiled=True) for e in each]  281 us
    pallas_call x1, Pallas kernels, last_layer(): call(functools.partial(last_layer_kernel, steps, bn), 12 * t * d * f, 4 *...  201 us
    pallas_call x1, Pallas kernels, reduce_scatter(): pl.pallas_call(functools.partial(reduce_kernel, n, chunks), in_specs=[pl....  138 us
    pallas_call x1, Pallas kernels, first_layer(): call(functools.partial(first_layer_kernel, steps, bn), 8 * t * d * f, 8 *...  136 us
    pallas_call x1, Pallas kernels, to_input(): call(to_input_kernel, 4 * t * d * f, 4 * t * f + 4 * d * f, 60, grid=(t /...  67.7 us
    pallas_call x1, Pallas kernels, gate_up(): call(gate_up_kernel, 4 * t * d * f, 10 * t * f + 4 * d * f, 56, grid=(f /...  62.2 us
    another operation x3, other arithmetic, step(): new[0].append(jnp.stack(gathered))  61.6 us
    pallas_call x1, Pallas kernels, down(): call(down_kernel, 2 * t * d * f, 2 * (t * f + d * f), 60, grid=(t // bm,)...  37 us
  transfers between devices with their start and end apart: 7, of which 6 were waited for; matrix products, arithmetic and copies ran while one was open for 9% of the time, Pallas kernels for 19%

profile of v1, /device:TPU:0, one launch (start us, length us, event | category | flops | bytes accessed | tf_op | source)
XLA Modules:
  0.0 1086.4 jit_solution(16484026652109838328)
XLA Ops:
  7.2 0.0 reduce-scatter.2.cloned.1.call-start
  7.2 3.2 fusion
  10.5 0.2 copy-done
  10.7 2.8 fusion.1.a_ref
  13.4 62.2 %gate_up.1 = (f32[2048,6144]{1,0:T(8,128)}, f32[2048,6144]{1,0:T(8,128)}, bf16[2048,6144]{1,0:T(8,128)(2,1)}) custom-call(bf16[2048,1024]{1,0:T(8,128)(2,1)} %fusion.1.a_ref, bf16[2,1024,6144]{2,1,0:T(8,128)(2,1)} %wg_ref.5, bf16[2,1024,6144]{2,1,0:T(8,128)(2,1)} %wu_ref.5), custom_call_target="tpu_custom_call" | custom-call | flops 51539607552 | bytes 150994944 | tf_op jit(solution)/shard_map/gate_up/pallas_call | solution.py:50
  75.6 37.0 %down.1 = (bf16[2048,1024]{1,0:T(8,128)(2,1)}, bf16[2048,1024]{1,0:T(8,128)(2,1)}) custom-call(bf16[2048,6144]{1,0:T(8,128)(2,1)} %get-tuple-element.21.act_ref, bf16[2,6144,1024]{2,1,0:T(8,128)(2,1)} %wd_ref.5, bf16[2048,1024]{1,0:T(8,128)(2,1)} %bitcast.111), custom_call_target="tpu_custom_call" | custom-call | flops 25769803776 | bytes 37748736 | tf_op jit(solution)/shard_map/down/pallas_call | solution.py:70
  112.6 201.5 %last_layer.1 = (bf16[2048,6144]{1,0:T(8,128)(2,1)}, bf16[2048,6144]{1,0:T(8,128)(2,1)}, bf16[16,18,64,1024]{3,2,1,0:T(8,128)(2,1)}) custom-call(bf16[2048,1024]{1,0:T(8,128)(2,1)} %get-tuple-element.22.a_ref, bf16[2048,1024]{1,0:T(8,128)(2,1)} %bitcast.124, bf16[2,1024,6144]{2,1,0:T(8,128)(2,1)} %wg_ref.5, bf16[2,1024,6144]{2,1,0:T(8,128)(2,1)} %wu_ref.5, ...), custom_call_target="tpu_custom_call" | custom-call | flops 154618822656 | bytes 125829120 | tf_op jit(solution)/shard_map/last_layer/pallas_call | solution.py:148
  314.1 0.0 reduce-scatter.2.cloned.1.call-update
  314.1 0.0 all-gather.9.cloned.1.call-start
  314.2 67.7 %to_input.1.dh_ref = bf16[2048,1024]{1,0:T(8,128)(2,1)} custom-call(bf16[2048,6144]{1,0:T(8,128)(2,1)} %get-tuple-element.23.dgate_ref, bf16[2048,6144]{1,0:T(8,128)(2,1)} %get-tuple-element.24.dup_ref, bf16[2,1024,6144]{2,1,0:T(8,128)(2,1)} %wg_ref.5, bf16[2,1024,6144]{2,1,0:T(8,128)(2,1)} %wu_ref.5, bf16[2048,1024]{1,0:T(8,128)(2,1)} %get-tuple-element.25.h_ref, ...), custom_call_target="tpu_custom_call" | custom-call | flops 51539607552 | bytes 75497472 | tf_op jit(solution)/shard_map/to_input/pallas_call | solution.py:176
  381.9 135.9 %first_layer.1 = bf16[16,18,64,1024]{3,2,1,0:T(8,128)(2,1)} custom-call(f32[2048,6144]{1,0:T(8,128)} %get-tuple-element.19.gate_ref, f32[2048,6144]{1,0:T(8,128)} %get-tuple-element.20.up_ref, bf16[2048,1024]{1,0:T(8,128)(2,1)} %fusion.1.a_ref, bf16[2048,1024]{1,0:T(8,128)(2,1)} %to_input.1.dh_ref, bf16[2,6144,1024]{2,1,0:T(8,128)(2,1)} %wd_ref.5), custom_call_target="tpu_custom_call" | custom-call | flops 103079215104 | bytes 150994944 | tf_op jit(solution)/shard_map/first_layer/pallas_call | solution.py:197
  517.9 1.2 reduce-scatter.2.cloned.1.call-done
  519.0 138.0 %reduce_scatter.12 = (bf16[18,64,1024]{2,1,0:T(8,128)(2,1)}, f32[8,128]{1,0:T(8,128)}) custom-call(bf16[2,2,2,2,18,64,1024]{6,5,4,3,2,1,0:T(8,128)(2,1)} %bitcast.126, bf16[18,64,1024]{2,1,0:T(8,128)(2,1)} %bitcast.123), custom_call_target="tpu_custom_call" | custom-call | flops 199999995904 | bytes 113246208 | tf_op jit(solution)/shard_map/reduce_scatter/pallas_call | solution.py:402
  657.1 1.3 reduce_sum.19
  659.1 4.2 fusion.57
  663.3 0.2 copy.28
  663.4 1.5 copy-done.13
  664.9 2.6 fusion.55
  667.5 0.1 copy.29
  667.7 0.5 copy-done.3
  668.1 1.5 copy-done.1
  669.6 3.7 fusion.4
  673.2 0.0 all-gather.9.cloned.1.call-update
  673.3 0.0 all-gather.7.cloned.1.call-start
  673.3 0.7 all-gather.7.cloned.1.call-update
  674.0 0.0 all-gather.13.cloned.1.call-start
  674.1 1.7 copy.30
  675.7 1.7 copy.31
  677.4 0.8 copy-done.5
  678.3 3.7 fusion.10
  681.9 0.0 all-gather.11.cloned.1.call-start
  682.0 0.5 all-gather.11.cloned.1.call-update
  682.5 0.0 all-gather.17.cloned.1.call-start
  682.6 4.9 fusion.16
  687.5 0.0 all-gather.15.cloned.1.call-start
  687.6 0.7 all-gather.15.cloned.1.call-update
  688.3 3.7 copy.20
  692.0 3.0 mul.614
  695.0 3.7 copy.21
  698.6 3.0 mul.616
  701.6 3.7 copy.22
  705.3 3.0 mul.618
  708.3 3.7 copy.23
  711.9 3.0 mul.620
  714.9 3.9 fusion.51
  718.9 3.8 pad_maximum_fusion.5
  722.7 1.3 copy-done.4
  723.9 0.4 copy-done.11
  724.4 0.5 copy-done.12
  724.8 1.5 multiply_add_fusion.3
  726.3 3.6 pad_maximum_fusion.3
  730.0 1.4 copy-done.8
  731.4 0.4 copy-done.9
  731.8 0.5 copy-done.10
  732.3 1.5 multiply_add_fusion.1
  733.8 3.1 pad_maximum_fusion.4
  736.9 64.0 %all-gather.7.cloned.1.call-done = bf16[1024,6144]{1,0:T(8,128)(2,1)} async-done(((bf16[64,6144]{1,0:T(8,128)(2,1)}), bf16[1024,6144]{1,0:T(8,128)(2,1)}) %all-gather.7.cloned.1.call-update) | async-done | bytes 12582928 | tf_op jit(solution)/shard_map/all_gather | solution.py:460
  800.9 20.5 %pad_maximum_fusion = bf16[2,1024,6144]{2,1,0:T(8,128)(2,1)} fusion(bf16[1,1024,6144]{2,1,0:T(8,128)(2,1)} %bitcast.113, bf16[1,1024,6144]{2,1,0:T(8,128)(2,1)} %bitcast.114), kind=kLoop, calls=%fused_computation | loop fusion | flops 12582912 | bytes 50331648 | tf_op jit(solution)/shard_map/stack | solution.py:461
  821.4 43.9 %all-gather.13.cloned.1.call-done = bf16[1024,6144]{1,0:T(8,128)(2,1)} async-done(((bf16[64,6144]{1,0:T(8,128)(2,1)}), bf16[1024,6144]{1,0:T(8,128)(2,1)}) %all-gather.13.cloned.1.call-update) | async-done | bytes 12582928 | tf_op jit(solution)/shard_map/all_gather | solution.py:460
  865.3 64.4 %all-gather.11.cloned.1.call-done = bf16[1024,6144]{1,0:T(8,128)(2,1)} async-done(((bf16[64,6144]{1,0:T(8,128)(2,1)}), bf16[1024,6144]{1,0:T(8,128)(2,1)}) %all-gather.11.cloned.1.call-update) | async-done | bytes 12582928 | tf_op jit(solution)/shard_map/all_gather | solution.py:460
  929.7 20.5 %pad_maximum_fusion.1 = bf16[2,1024,6144]{2,1,0:T(8,128)(2,1)} fusion(bf16[1,1024,6144]{2,1,0:T(8,128)(2,1)} %bitcast.115, bf16[1,1024,6144]{2,1,0:T(8,128)(2,1)} %bitcast.116), kind=kLoop, calls=%fused_computation.1 | loop fusion | flops 12582912 | bytes 50331648 | tf_op jit(solution)/shard_map/stack | solution.py:461
  950.3 43.9 %all-gather.17.cloned.1.call-done = bf16[6144,1024]{1,0:T(8,128)(2,1)} async-done(((bf16[384,1024]{1,0:T(8,128)(2,1)}), bf16[6144,1024]{1,0:T(8,128)(2,1)}) %all-gather.17.cloned.1.call-update) | async-done | bytes 12582928 | tf_op jit(solution)/shard_map/all_gather | solution.py:460
  994.1 64.6 %all-gather.15.cloned.1.call-done = bf16[6144,1024]{1,0:T(8,128)(2,1)} async-done(((bf16[384,1024]{1,0:T(8,128)(2,1)}), bf16[6144,1024]{1,0:T(8,128)(2,1)}) %all-gather.15.cloned.1.call-update) | async-done | bytes 12582928 | tf_op jit(solution)/shard_map/all_gather | solution.py:460
  1058.7 20.5 %pad_maximum_fusion.2 = bf16[2,6144,1024]{2,1,0:T(8,128)(2,1)} fusion(bf16[1,6144,1024]{2,1,0:T(8,128)(2,1)} %bitcast.117, bf16[1,6144,1024]{2,1,0:T(8,128)(2,1)} %bitcast.118), kind=kLoop, calls=%fused_computation.2 | loop fusion | flops 12582912 | bytes 50331648 | tf_op jit(solution)/shard_map/stack | solution.py:461
  (21 shorter events, 0.1 us)
Async XLA Ops:
  7.2 511.9 %reduce-scatter.2.cloned.1.call-start = ((), (), s32[]{:S(2)}) async-start(), calls=%async_computation.1 | async-start | bytes 40108032 | tf_op jit(solution)/shard_map/reduce_scatter | solution.py:446
  7.2 3.5 copy-start
  314.1 422.8 %all-gather.9.cloned.1.call-start = ((), (), s32[]{:S(2)}) async-start(), calls=%async_computation.3 | async-start | bytes 13369344 | tf_op jit(solution)/shard_map/all_gather | solution.py:460
  663.3 1.7 copy-start.13
  664.9 3.2 copy-start.3
  667.5 2.0 copy-start.1
  673.3 127.7 %all-gather.7.cloned.1.call-start = ((), (), s32[]{:S(2)}) async-start(), calls=%async_computation.2 | async-start | bytes 13369344 | tf_op jit(solution)/shard_map/all_gather | solution.py:460
  674.0 191.3 %all-gather.13.cloned.1.call-start = ((), (), s32[]{:S(2)}) async-start(), calls=%async_computation.5 | async-start | bytes 13369344 | tf_op jit(solution)/shard_map/all_gather | solution.py:460
  674.0 3.4 copy-start.7
  675.7 2.5 copy-start.5
  681.9 247.8 %all-gather.11.cloned.1.call-start = ((), (), s32[]{:S(2)}) async-start(), calls=%async_computation.4 | async-start | bytes 13369344 | tf_op jit(solution)/shard_map/all_gather | solution.py:460
  682.5 311.6 %all-gather.17.cloned.1.call-start = ((), (), s32[]{:S(2)}) async-start(), calls=%async_computation.7 | async-start | bytes 13369344 | tf_op jit(solution)/shard_map/all_gather | solution.py:460
  687.5 371.1 %all-gather.15.cloned.1.call-start = ((), (), s32[]{:S(2)}) async-start(), calls=%async_computation.6 | async-start | bytes 13369344 | tf_op jit(solution)/shard_map/all_gather | solution.py:460
  718.8 3.8 copy-start.2
  718.8 5.1 copy-start.4
  718.8 5.5 copy-start.11
  718.9 6.0 copy-start.12
  726.3 3.7 copy-start.6
  726.3 5.1 copy-start.8
  726.3 5.5 copy-start.9
  726.3 6.0 copy-start.10
Sparse Core Ops, SparseCore 0:
  314.2 204.7 reduce-scatter.1
  673.4 62.3 all-gather.8
  738.6 62.2 all-gather.6
  803.0 62.2 all-gather.12
  867.4 62.2 all-gather.10
  931.8 62.2 all-gather.16
  996.4 62.2 all-gather.14

commit v2 on v1

--- a/solution.py
+++ b/solution.py
@@ -34,47 +34,52 @@
     return (wide * lax.rsqrt(jnp.mean(wide * wide, -1, keepdims=True) + EPS)).astype(BF16)
 
 
-def gate_up_kernel(a_ref, wg_ref, wu_ref, gate_ref, up_ref, act_ref):
-    gate = dot(a_ref[...], wg_ref[0], 1, 0)
-    up = dot(a_ref[...], wu_ref[0], 1, 0)
-    gate_ref[...] = gate
-    up_ref[...] = up
-    act_ref[...] = (gate * jax.nn.sigmoid(gate) * up).astype(BF16)
-
-
-def gate_up(a, wg, wu, bn=256):
-    t, d = a.shape
+def first_forward_kernel(steps, parts, x_ref, wg_ref, wu_ref, wd_ref, gate_ref, up_ref, a_ref, h_ref, next_ref, total):
+    k = pl.program_id(0)
+    t = x_ref.shape[0]
+
+    @pl.when(k == 0)
+    def _():
+        total[...] = jnp.zeros_like(total)
+
+        @pl.loop(0, 8)
+        def _(i):
+            r = pl.ds(i * (t // 8), t // 8)
+            a_ref[r, :] = normed(x_ref[r, :])
+
+    for i in range(parts):
+        r = pl.ds(i * (t // parts), t // parts)
+        gate = dot(a_ref[r, :], wg_ref[0], 1, 0)
+        up = dot(a_ref[r, :], wu_ref[0], 1, 0)
+        gate_ref[r, :] = gate
+        up_ref[r, :] = up
+        total[r, :] += dot((gate * jax.nn.sigmoid(gate) * up).astype(BF16), wd_ref[0], 1, 0)
+
+    @pl.when(k == steps - 1)
+    def _():
+        @pl.loop(0, 8)
+        def _(i):
+            r = pl.ds(i * (t // 8), t // 8)
+            h = x_ref[r, :] + total[r, :].astype(BF16)
+            h_ref[r, :] = h
+            next_ref[r, :] = normed(h)
+
+
+def first_forward(x, wg, wu, wd, bn=512, parts=2):
+    t, d = x.shape
     f = wg.shape[2]
+    steps = f // bn
     w = pl.BlockSpec((1, d, bn), lambda j: (0, 0, j))
     o = pl.BlockSpec((t, bn), lambda j: (0, j))
     return call(
-        gate_up_kernel, 4 * t * d * f, 10 * t * f + 4 * d * f, 56,
-        grid=(f // bn,),
-        in_specs=[whole(t, d), w, w],
-        out_specs=[o, o, o],
-        out_shape=[jax.ShapeDtypeStruct((t, f), F32)] * 2 + [jax.ShapeDtypeStruct((t, f), BF16)],
-        name="gate_up",
-    )(a, wg, wu)
-
-
-def down_kernel(act_ref, wd_ref, x_ref, h_ref, a_ref):
-    h = x_ref[...] + dot(act_ref[...], wd_ref[0], 1, 0).astype(BF16)
-    h_ref[...] = h
-    a_ref[...] = normed(h)
-
-
-def down(act, wd, x, bm=512):
-    t, f = act.shape
-    d = x.shape[1]
-    r = pl.BlockSpec((bm, d), lambda i: (i, 0))
-    return call(
-        down_kernel, 2 * t * d * f, 2 * (t * f + d * f), 60,
-        grid=(t // bm,),
-        in_specs=[pl.BlockSpec((bm, f), lambda i: (i, 0)), whole(1, f, d), r],
-        out_specs=[r, r],
-        out_shape=[jax.ShapeDtypeStruct((t, d), BF16)] * 2,
-        name="down",
-    )(act, wd, x)
+        functools.partial(first_forward_kernel, steps, parts), 6 * t * d * f, 8 * t * f + 6 * d * f, 63,
+        grid=(steps,),
+        in_specs=[whole(t, d), w, w, pl.BlockSpec((1, bn, d), lambda j: (0, j, 0))],
+        out_specs=[o, o] + [whole(t, d)] * 3,
+        out_shape=[jax.ShapeDtypeStruct((t, f), F32)] * 2 + [jax.ShapeDtypeStruct((t, d), BF16)] * 3,
+        scratch_shapes=[pltpu.VMEM((t, d), F32)],
+        name="first_forward",
+    )(x, wg, wu, wd)
 
 
 def back_through_product(gate, up, dact):
@@ -128,17 +133,19 @@
     ]
 
 
-def last_layer_kernel(steps, bn, a_ref, dy_ref, wg_ref, wu_ref, wd_ref, dgate_ref, dup_ref, p_ref, *scratch):
-    gate = dot(a_ref[...], wg_ref[0], 1, 0)
-    up = dot(a_ref[...], wu_ref[0], 1, 0)
-    dact = dot(dy_ref[...], wd_ref[0], 1, 1)
-    act, dgate, dup = back_through_product(gate, up, dact)
-    dgate_ref[...] = dgate
-    dup_ref[...] = dup
-    put_terms(p_ref, *scratch, pl.program_id(0), steps, act, dgate, dup, a_ref, dy_ref, bn)
-
-
-def last_layer(a, dy, wg, wu, wd, n, bn=512):
+def last_layer_kernel(steps, bn, parts, a_ref, dy_ref, wg_ref, wu_ref, wd_ref, dgate_ref, dup_ref, p_ref, act, *scratch):
+    t = a_ref.shape[0]
+    for i in range(parts):
+        r = pl.ds(i * (t // parts), t // parts)
+        gate = dot(a_ref[r, :], wg_ref[0], 1, 0)
+        up = dot(a_ref[r, :], wu_ref[0], 1, 0)
+        dact = dot(dy_ref[r, :], wd_ref[0], 1, 1)
+        act[r, :], dgate_ref[r, :], dup_ref[r, :] = back_through_product(gate, up, dact)
+    terms_of = act[...], dgate_ref[...], dup_ref[...]
+    put_terms(p_ref, *scratch, pl.program_id(0), steps, *terms_of, a_ref, dy_ref, bn)
+
+
+def last_layer(a, dy, wg, wu, wd, n, bn=512, parts=2):
     t, d = a.shape
     f = wg.shape[2]
     last = wg.shape[0] - 1
@@ -146,12 +153,12 @@
     w = pl.BlockSpec((1, d, bn), lambda j: (last, 0, j))
     o = pl.BlockSpec((t, bn), lambda j: (0, j))
     return call(
-        functools.partial(last_layer_kernel, steps, bn), 12 * t * d * f, 4 * t * f + 12 * d * f, 60,
+        functools.partial(last_layer_kernel, steps, bn, parts), 12 * t * d * f, 4 * t * f + 12 * d * f, 63,
         grid=(steps,),
         in_specs=[whole(t, d), whole(t, d), w, w, pl.BlockSpec((1, bn, d), lambda j: (last, j, 0))],
         out_specs=[o, o, pl.BlockSpec(memory_space=pl.ANY)],
         out_shape=[jax.ShapeDtypeStruct((t, f), BF16)] * 2 + [jax.ShapeDtypeStruct((n, 3 * f // n // 64, 64, d), BF16)],
-        scratch_shapes=term_scratch(n, d, bn),
+        scratch_shapes=[pltpu.VMEM((t, bn), BF16)] + term_scratch(n, d, bn),
         name="last_layer",
     )(a, dy, wg, wu, wd)
 
@@ -294,6 +301,7 @@
 
     @pl.loop(0, g1_ref.shape[0])
     def _(b):
+        g_ref[1, b] = g1_ref[b]
         wide = g1_ref[b].astype(F32)
         square[...] += fold(wide * wide)
 
@@ -337,7 +345,7 @@
                 *_, mine, mine_in_a, mine_in_b = indices(q)
                 o, k, ka, kb = (lax.rem(i, slots), q) + mine, (i, q) + mine, (i, q) + mine_in_a, (i, q) + mine_in_b
                 g = add([own[o], from_core[k], from_a[ka], from_b[kb], from_c[i, q]]).astype(BF16)
-                g_ref[q * chunks + i] = g
+                g_ref[0, q * chunks + i] = g
                 wide = g.astype(F32)
                 square[...] += fold(wide * wide)
 
@@ -403,7 +411,7 @@
         functools.partial(reduce_kernel, n, chunks),
         in_specs=[pl.BlockSpec(memory_space=pl.ANY), pl.BlockSpec(memory_space=pltpu.VMEM)],
         out_specs=[pl.BlockSpec(memory_space=pltpu.VMEM)] * 2,
-        out_shape=[jax.ShapeDtypeStruct((blocks, rows, d), BF16), jax.ShapeDtypeStruct((8, 128), F32)],
+        out_shape=[jax.ShapeDtypeStruct((2, blocks, rows, d), BF16), jax.ShapeDtypeStruct((8, 128), F32)],
         scratch_shapes=[
             cells(4, 3, 2, 2, 2), cells(chunks, 3, 2, 2, 2), cells(chunks, 3, 2, 2), cells(chunks, 3, 2), cells(chunks, 3),
             pltpu.VMEM((8, 128), F32), pltpu.VMEM((n, 8, 128), F32), sem((4, 3)),
@@ -414,54 +422,167 @@
     )(p.reshape(2, 2, 2, 2, blocks, rows, d), g1)
 
 
-def adamw(w, m, v, g):
-    m = 0.9 * m + 0.1 * g
-    v = 0.95 * v + 0.05 * g * g
-    step = m * lax.rsqrt(v + 1e-8) + 0.1 * w
-    return (w - 0.02 * step).astype(BF16), m, v
+def moments_of(m, v, g):
+    return 0.9 * m + 0.1 * g, 0.95 * v + 0.05 * g * g
+
+
+def factor_of(sq_ref, count):
+    square = jnp.sum(sq_ref[...], keepdims=True)
+    return jnp.minimum(1.0, 0.5 * lax.rsqrt(square / count + 1e-30))
+
+
+def new_weights_kernel(count, me_ref, sq_ref, *refs):
+    factor = factor_of(sq_ref, count)
+    for i in range(3):
+        m_ref, v_ref, g_ref, w_ref, out_ref = refs[i::3]
+        m, v = moments_of(m_ref[0], v_ref[0], g_ref[0, 0].astype(F32) * factor)
+        w = w_ref[0].astype(F32)
+        out_ref[0] = (w - 0.02 * (m * lax.rsqrt(v + 1e-8) + 0.1 * w)).astype(BF16)
+
+
+def new_moments_kernel(count, me_ref, sq_ref, *refs):
+    factor = factor_of(sq_ref, count)
+    for i in range(3):
+        m_ref, v_ref, g_ref, new_m_ref, new_v_ref = refs[i::3]
+        new_m_ref[0], new_v_ref[0] = moments_of(m_ref[0], v_ref[0], g_ref[0, 0].astype(F32) * factor)
+
+
+def update(kernel, name, me, squares, m, v, g, count, w, dtypes):
+    layers, blocks, rows, d = g.shape
+    per = blocks // 3
+    wide = lambda row: pl.BlockSpec((1, rows, d), lambda l, j, me: (l, row(me), j))
+    tall = lambda first: pl.BlockSpec((1, rows, d), lambda l, j, me: (l, first(me) + j, 0))
+    zero, own = (lambda me: 0), (lambda me: me[0])
+    in_place = [wide(zero), wide(zero), tall(zero)]
+    of_g = [pl.BlockSpec((1, 1, rows, d), lambda l, j, me, k=k: (l, k * per + j, 0, 0)) for k in (1, 2, 0)]
+    of_w = [wide(own), wide(own), tall(lambda me: me[0] * per)] if w else []
+    return pl.pallas_call(
+        functools.partial(kernel, float(count)),
+        grid_spec=pltpu.PrefetchScalarGridSpec(
+            num_scalar_prefetch=1,
+            grid=(layers, per),
+            in_specs=[pl.BlockSpec((8, 128), lambda l, j, me: (0, 0))] + in_place * 2 + of_g + of_w,
+            out_specs=in_place * len(dtypes),
+        ),
+        out_shape=[jax.ShapeDtypeStruct(a.shape, dtype) for dtype in dtypes for a in m],
+        compiler_params=pltpu.CompilerParams(vmem_limit_bytes=60 * MIB, dimension_semantics=("arbitrary",) * 2),
+        cost_estimate=pl.CostEstimate(flops=20_000_000_000, bytes_accessed=20 * sum(a.size for a in m), transcendentals=0),
+        name=name,
+    )(me, squares, *m, *v, g, g, g, *w)
+
+
+def copy_kernel(a_ref, b_ref, a_out, b_out):
+    a_out[...] = a_ref[...]
+    b_out[...] = b_ref[...]
+
+
+def copied(a, b, rows=256):
+    layers, n, columns = a.shape
+    block = pl.BlockSpec((1, rows, columns), lambda l, i: (l, i, 0))
+    return pl.pallas_call(
+        copy_kernel,
+        grid=(layers, n // rows),
+        in_specs=[block] * 2,
+        out_specs=[block] * 2,
+        out_shape=[jax.ShapeDtypeStruct(a.shape, a.dtype)] * 2,
+        compiler_params=pltpu.CompilerParams(vmem_limit_bytes=60 * MIB, dimension_semantics=("arbitrary",) * 2),
+        cost_estimate=pl.CostEstimate(flops=20_000_000_000, bytes_accessed=8 * a.size, transcendentals=0),
+        name="copied",
+    )(a, b)
+
+
+def gather_kernel(n, layers, pieces, gate_ref, up_ref, full_gate, full_up, own_sem, *sems):
+    me, bits, core = place()
+    partner = {"dp": me + 1 - 2 * core}
+    width = gate_ref.shape[2] // (3 * pieces)
+    chunks = [(l, k, which) for l in range(layers) for k in range(pieces) for which in range(2)]
+    mine = (gate_ref, up_ref)
+    full = (full_gate, full_up)
+    greet_all(me, n)
+
+    def region(i, q, free):
+        l, k, which = chunks[i]
+        lead = tuple(slice(None) if a in free else bits[a] for a in range(3))
+        return full[which].at[(l,) + lead + (core, slice(None), pl.ds((3 * k + q) * width, width))]
+
+    def source(i, q):
+        l, k, which = chunks[i]
+        return mine[which].at[l, :, pl.ds((3 * k + q) * width, width)]
+
+    def own_copy(i, q):
+        return pltpu.make_async_copy(source(i, q), region(i, q, ()), own_sem.at[i, q])
+
+    def copy(i, q, stage):
+        order = ORDERS[q]
+        part = region(i, q, order[:stage])
+        return pltpu.make_async_remote_copy(
+            src_ref=source(i, q) if stage == 0 else part, dst_ref=part,
+            send_sem=sems[2 * stage].at[i, q], recv_sem=sems[2 * stage + 1].at[i, q],
+            device_id=partner if stage == 3 else neighbour(me, bits, order[stage]), device_id_type=MESH,
+        )
+
+    for s in range(len(chunks) + 3):
+        for stage in range(4):
+            i = s - stage
+            if 0 <= i < len(chunks):
+                for q in range(3):
+                    if stage == 0:
+                        own_copy(i, q).start()
+                    else:
+                        copy(i, q, stage - 1).wait_recv()
+                        if stage == 1:
+                            own_copy(i, q).wait()
+                    copy(i, q, stage).start()
+    for i in range(len(chunks)):
+        for q in range(3):
+            for stage in range(4):
+                copy(i, q, stage).wait_send()
+            copy(i, q, 3).wait_recv()
+
+
+def gather(gate, up, n, pieces=2):
+    layers, rows, columns = gate.shape
+    sem = pltpu.SemaphoreType.DMA
+    chunks = layers * pieces * 2
+    full = jax.ShapeDtypeStruct((layers, 2, 2, 2, 2, rows, columns), BF16)
+    out = pl.pallas_call(
+        functools.partial(gather_kernel, n, layers, pieces),
+        in_specs=[pl.BlockSpec(memory_space=pltpu.VMEM)] * 2,
+        out_specs=[pl.BlockSpec(memory_space=pl.ANY)] * 2,
+        out_shape=[full] * 2,
+        scratch_shapes=[sem((chunks, 3))] * 9,
+        compiler_params=pltpu.CompilerParams(vmem_limit_bytes=60 * MIB, collective_id=1, has_side_effects=True),
+        cost_estimate=pl.CostEstimate(flops=200_000_000_000, bytes_accessed=6 * n * gate.size, transcendentals=0),
+        name="gather",
+    )(gate, up)
+    return [o.reshape(layers, n * rows, columns) for o in out]
 
 
 def terms(x, dy, wg, wu, wd, n):
-    a0 = normed(x)
-    gate, up, act = gate_up(a0, wg, wu)
-    h1, a1 = down(act, wd, x)
+    gate, up, a0, h1, a1 = first_forward(x, wg, wu, wd)
     dgate, dup, p1 = last_layer(a1, dy, wg, wu, wd, n)
     dh = to_input(dgate, dup, wg, wu, h1, dy)
     p0 = first_layer(gate, up, a0, dh, wd, n)
     return p1, p0
 
 
-def unpacked(g, blocks):
-    wide = lambda t: t.transpose(1, 0, 2).reshape(64, -1)
-    return wide(g[blocks : 2 * blocks]), wide(g[2 * blocks :]), g[:blocks].reshape(-1, g.shape[-1])
-
-
 def solution(mesh):
     n = mesh.shape["dp"]
 
     def step(x, dy, *arrays):
         w, m, v = (arrays[i : i + 3] for i in (0, 3, 6))
-        packed = terms(x[0], dy[0], *w, n)
-        blocks = packed[0].shape[1] // 3
-        g1 = lax.psum_scatter(packed[0], "dp", scatter_dimension=0, tiled=True)[0]
-        g0, squares = reduce_scatter(packed[1], g1)
-        by_layer = [[g.astype(F32) for g in unpacked(s, blocks)] for s in (g0, g1)]
+        p1, p0 = terms(x[0], dy[0], *w, n)
+        g1 = lax.psum_scatter(p1, "dp", scatter_dimension=0, tiled=True)[0]
+        g, squares = reduce_scatter(p0, g1)
+        me = lax.axis_index("dp").astype(jnp.int32).reshape(1)
         count = sum(a.size for a in w)
-        square = jnp.sum(squares)
-        factor = jnp.minimum(1.0, 0.5 * lax.rsqrt(square / count + 1e-30))
-        me = lax.axis_index("dp")
-        new = [[], [], []]
-        for i in range(3):
-            rows = m[i].shape[1]
-            each = []
-            for layer in range(2):
-                own = lax.dynamic_slice(w[i], (layer, me * rows, 0), (1, rows, w[i].shape[2]))[0].astype(F32)
-                each.append(adamw(own, m[i][layer], v[i][layer], by_layer[layer][i] * factor))
-            gathered = [lax.all_gather(e[0], "dp", axis=0, tiled=True) for e in each]
-            new[0].append(jnp.stack(gathered))
-            new[1].append(jnp.stack([e[1] for e in each]))
-            new[2].append(jnp.stack([e[2] for e in each]))
-        return tuple(new[0] + new[1] + new[2])
+        gate, up, down_ = update(new_weights_kernel, "new_weights", me, squares, m, v, g, count, w, [BF16])
+        gate, up = gather(gate, up, n)
+        gate, up, down_, g = lax.optimization_barrier((gate, up, down_, g))
+        down_ = lax.all_gather(down_, "dp", axis=1, tiled=True)
+        gate, up = copied(gate, up)
+        moments = update(new_moments_kernel, "new_moments", me, squares, m, v, g, count, (), [F32] * 2)
+        return gate, up, down_, *moments
 
     rows, all_ = P("dp"), P()
     moment, out_moment = P(None, "dp"), P("rep", "dp")

time: 1090 us -> 956 us (0.88)
  waiting for transfers between devices: 284 us -> 52.7 us
  Pallas kernels: 642 us -> 863 us
  other arithmetic: 105 us -> 0 us
  local copies, waits for them, and re-layouts: 39.2 us -> 20.7 us
    all_gather x6 -> x1, waiting for transfers between devices: 281 us -> 51.7 us  [step(): down_ = lax.all_gather(down_, 'dp', axis=1, tiled=True)]
    pallas_call x3 -> x6, Pallas kernels: 301 us -> 520 us  [the longest x1 186 us: last_layer(): call(functools.partial(last_layer_kernel, steps, bn, parts), 12 * t * d *...]
    another operation x6 -> x0, other arithmetic: 72.1 us -> none  [the longest x3 61.6 us: step(): new[0].append(jnp.stack(gathered))]
    mul x12 -> x0, local copies, waits for them, and re-layouts: 30.2 us -> none  [step(): by_layer[layer][i] * factor]
    convert_element_type x4 -> x0, other arithmetic: 15 us -> none  [the longest x3 12.3 us: adamw(): return ((w - 0.02 * step).astype(BF16), m, v)]
    unnamed x28 -> x1, local copies, waits for them, and re-layouts: 8.99 us -> 20.7 us
  transfers between devices with their start and end apart: 7 -> 2, of which waited for: 6 -> 2; matrix products, arithmetic and copies ran while one was open for 9% -> 0% of each run, Pallas kernels for 19% -> 27%
where the time goes in v2:
time: 956 us; the launch traced here: 951 us
  Pallas kernels  863 us (90%)
  waiting for transfers between devices  52.7 us (6%)
  local copies, waits for them, and re-layouts  20.7 us (2%)
  between operations  14.5 us (2%)
    pallas_call x1, Pallas kernels, last_layer(): call(functools.partial(last_layer_kernel, steps, bn, parts), 12 * t * d *...  186 us
    pallas_call x1, Pallas kernels, gather(): pl.pallas_call(functools.partial(gather_kernel, n, layers, pieces), in_sp...  171 us
    pallas_call x1, Pallas kernels, reduce_scatter(): pl.pallas_call(functools.partial(reduce_kernel, n, chunks), in_specs=[pl....  139 us
    pallas_call x1, Pallas kernels, first_layer(): call(functools.partial(first_layer_kernel, steps, bn), 8 * t * d * f, 8 *...  136 us
    pallas_call x1, Pallas kernels, first_forward(): call(functools.partial(first_forward_kernel, steps, parts), 6 * t * d * f...  95.8 us
    pallas_call x1, Pallas kernels, to_input(): call(to_input_kernel, 4 * t * d * f, 4 * t * f + 4 * d * f, 60, grid=(t /...  67.9 us
    all_gather x1, waiting for transfers between devices, step(): down_ = lax.all_gather(down_, 'dp', axis=1, tiled=True)  51.7 us
    pallas_call x2, Pallas kernels, update(): pl.pallas_call(functools.partial(kernel, float(count)), grid_spec=pltpu.P...  34.8 us
  transfers between devices with their start and end apart: 2, of which 2 were waited for; matrix products, arithmetic and copies ran while one was open for 0% of the time, Pallas kernels for 27%

profile of v2, /device:TPU:0, one launch (start us, length us, event | category | flops | bytes accessed | tf_op | source)
XLA Modules:
  0.0 950.8 jit_solution(6659120939753552390)
XLA Ops:
  7.2 0.0 reduce-scatter.2.cloned.1.call-start
  7.2 95.8 %first_forward.1 = (f32[2048,6144]{1,0:T(8,128)}, f32[2048,6144]{1,0:T(8,128)}, bf16[2048,1024]{1,0:T(8,128)(2,1)}, bf16[2048,1024]{1,0:T(8,128)(2,1)}, bf16[2048,1024]{1,0:T(8,128)(2,1)}) custom-call(bf16[2048,1024]{1,0:T(8,128)(2,1)} %bitcast.7, bf16[2,1024,6144]{2,1,0:T(8,128)(2,1)} %refs_9_.1, bf16[2,1024,6144]{2,1,0:T(8,128)(2,1)} %refs_10_.1, ...), custom_call_target="tpu_custom_call" | custom-call | flops 77309411328 | bytes 138412032 | tf_op jit(solution)/shard_map/first_forward/pallas_call | solution.py:74
  103.0 186.0 %last_layer.1 = (bf16[2048,6144]{1,0:T(8,128)(2,1)}, bf16[2048,6144]{1,0:T(8,128)(2,1)}, bf16[16,18,64,1024]{3,2,1,0:T(8,128)(2,1)}) custom-call(bf16[2048,1024]{1,0:T(8,128)(2,1)} %get-tuple-element.39.a_ref, bf16[2048,1024]{1,0:T(8,128)(2,1)} %bitcast.8, bf16[2,1024,6144]{2,1,0:T(8,128)(2,1)} %refs_9_.1, bf16[2,1024,6144]{2,1,0:T(8,128)(2,1)} %refs_10_.1, ...), custom_call_target="tpu_custom_call" | custom-call | flops 154618822656 | bytes 125829120 | tf_op jit(solution)/shard_map/last_layer/pallas_call | solution.py:155
  289.0 0.0 reduce-scatter.2.cloned.1.call-update
  289.1 0.0 all-gather.2.cloned.1.call-start
  289.1 67.9 %to_input.1.dh_ref = bf16[2048,1024]{1,0:T(8,128)(2,1)} custom-call(bf16[2048,6144]{1,0:T(8,128)(2,1)} %get-tuple-element.40.dgate_ref, bf16[2048,6144]{1,0:T(8,128)(2,1)} %get-tuple-element.41.dup_ref, bf16[2,1024,6144]{2,1,0:T(8,128)(2,1)} %refs_9_.1, bf16[2,1024,6144]{2,1,0:T(8,128)(2,1)} %refs_10_.1, bf16[2048,1024]{1,0:T(8,128)(2,1)} %get-tuple-element.42.h_ref, ...), custom_call_target="tpu_custom_call" | custom-call | flops 51539607552 | bytes 75497472 | tf_op jit(solution)/shard_map/to_input/pallas_call | solution.py:183
  357.0 136.0 %first_layer.1 = bf16[16,18,64,1024]{3,2,1,0:T(8,128)(2,1)} custom-call(f32[2048,6144]{1,0:T(8,128)} %get-tuple-element.36.gate_ref, f32[2048,6144]{1,0:T(8,128)} %get-tuple-element.37.up_ref, bf16[2048,1024]{1,0:T(8,128)(2,1)} %get-tuple-element.38.a_ref, bf16[2048,1024]{1,0:T(8,128)(2,1)} %to_input.1.dh_ref, bf16[2,6144,1024]{2,1,0:T(8,128)(2,1)} %refs_11_.1), custom_call_target="tpu_custom_call" | custom-call | flops 103079215104 | bytes 150994944 | tf_op jit(solution)/shard_map/first_layer/pallas_call | solution.py:204
  493.1 0.9 reduce-scatter.2.cloned.1.call-done
  494.0 138.8 %reduce_scatter.12 = (bf16[2,18,64,1024]{3,2,1,0:T(8,128)(2,1)}, f32[8,128]{1,0:T(8,128)}) custom-call(bf16[2,2,2,2,18,64,1024]{6,5,4,3,2,1,0:T(8,128)(2,1)} %bitcast.11, bf16[18,64,1024]{2,1,0:T(8,128)(2,1)} %bitcast.10), custom_call_target="tpu_custom_call" | custom-call | flops 199999995904 | bytes 113246208 | tf_op jit(solution)/shard_map/reduce_scatter/pallas_call | solution.py:410
  632.9 17.0 %new_weights.1 = (bf16[2,64,6144]{2,1,0:T(8,128)(2,1)}, bf16[2,64,6144]{2,1,0:T(8,128)(2,1)}, bf16[2,384,1024]{2,1,0:T(8,128)(2,1)}) custom-call(s32[1]{0:T(128)} %bitcast.me_ref, f32[8,128]{1,0:T(8,128)} %get-tuple-element.44.sq_ref, f32[2,64,6144]{2,1,0:T(8,128)} %refs_0_.3, f32[2,64,6144]{2,1,0:T(8,128)} %refs_1_.3, f32[2,384,1024]{2,1,0:T(8,128)} %refs_2_.3, ...), custom_call_target="tpu_custom_call" | custom-call | flops 20000000000 | bytes 47185920 | tf_op jit(solution)/shard_map/new_weights/pallas_call | solution.py:459
  649.9 171.1 %gather.1 = (bf16[2,2,2,2,2,64,6144]{6,5,4,3,2,1,0:T(8,128)(2,1)}, bf16[2,2,2,2,2,64,6144]{6,5,4,3,2,1,0:T(8,128)(2,1)}) custom-call(bf16[2,64,6144]{2,1,0:T(8,128)(2,1)} %get-tuple-element.46.gate_ref, bf16[2,64,6144]{2,1,0:T(8,128)(2,1)} %get-tuple-element.47.up_ref), custom_call_target="tpu_custom_call" | custom-call | flops 199999995904 | bytes 75497472 | tf_op jit(solution)/shard_map/gather/pallas_call | solution.py:548
  821.0 0.0 all-gather.2.cloned.1.call-update
  821.0 17.8 %new_moments.1 = (f32[2,64,6144]{2,1,0:T(8,128)}, f32[2,64,6144]{2,1,0:T(8,128)}, f32[2,384,1024]{2,1,0:T(8,128)}, f32[2,64,6144]{2,1,0:T(8,128)}, f32[2,64,6144]{2,1,0:T(8,128)}, /*index=5*/f32[2,384,1024]{2,1,0:T(8,128)}) custom-call(s32[1]{0:T(128)} %bitcast.me_ref, f32[8,128]{1,0:T(8,128)} %get-tuple-element.44.sq_ref, f32[2,64,6144]{2,1,0:T(8,128)} %refs_0_.3, ...), custom_call_target="tpu_custom_call" | custom-call | flops 20000000000 | bytes 47185920 | tf_op jit(solution)/shard_map/new_moments/pallas_call | solution.py:459
  838.8 32.4 %copied.1 = (bf16[2,1024,6144]{2,1,0:T(8,128)(2,1)}, bf16[2,1024,6144]{2,1,0:T(8,128)(2,1)}) custom-call(bf16[2,1024,6144]{2,1,0:T(8,128)(2,1)} %bitcast.12, bf16[2,1024,6144]{2,1,0:T(8,128)(2,1)} %bitcast.13), custom_call_target="tpu_custom_call" | custom-call | flops 20000000000 | bytes 100663296 | tf_op jit(solution)/shard_map/copied/pallas_call | solution.py:482
  871.1 51.7 %all-gather.2.cloned.1.call-done = bf16[2,6144,1024]{2,1,0:T(8,128)(2,1)} async-done(((bf16[2,384,1024]{2,1,0:T(8,128)(2,1)}), bf16[2,6144,1024]{2,1,0:T(8,128)(2,1)}) %all-gather.2.cloned.1.call-update) | async-done | bytes 25165840 | tf_op jit(solution)/shard_map/all_gather | solution.py:582
  922.9 20.7 %copy.21 = bf16[2,6144,1024]{2,1,0:T(8,128)(2,1)} copy(bf16[2,6144,1024]{2,1,0:T(8,128)(2,1)} %all-gather.2.cloned.1.call-done) | data formatting | bytes 50331648
Async XLA Ops:
  7.2 486.8 %reduce-scatter.2.cloned.1.call-start = ((), (), s32[]{:S(2)}) async-start(), calls=%async_computation.1 | async-start | bytes 40108032 | tf_op jit(solution)/shard_map/reduce_scatter | solution.py:575
  289.1 633.8 %all-gather.2.cloned.1.call-start = ((), (), s32[]{:S(2)}) async-start(), calls=%async_computation.2 | async-start | bytes 26738688 | tf_op jit(solution)/shard_map/all_gather | solution.py:582
Sparse Core Ops, SparseCore 0:
  289.2 204.7 reduce-scatter.1
  821.1 101.6 all-gather.1

commit v3 on v2

--- a/solution.py
+++ b/solution.py
@@ -431,30 +431,38 @@
     return jnp.minimum(1.0, 0.5 * lax.rsqrt(square / count + 1e-30))
 
 
+def tiles(i, g_ref):
+    _, count, rows, d = g_ref.shape
+    for b in range(count):
+        yield b, ((0, pl.ds(b * rows, rows), slice(None)) if i == 2 else (0, slice(None), pl.ds(b * d, d)))
+
+
 def new_weights_kernel(count, me_ref, sq_ref, *refs):
     factor = factor_of(sq_ref, count)
     for i in range(3):
         m_ref, v_ref, g_ref, w_ref, out_ref = refs[i::3]
-        m, v = moments_of(m_ref[0], v_ref[0], g_ref[0, 0].astype(F32) * factor)
-        w = w_ref[0].astype(F32)
-        out_ref[0] = (w - 0.02 * (m * lax.rsqrt(v + 1e-8) + 0.1 * w)).astype(BF16)
+        for b, at_ in tiles(i, g_ref):
+            m, v = moments_of(m_ref[at_], v_ref[at_], g_ref[0, b].astype(F32) * factor)
+            w = w_ref[at_].astype(F32)
+            out_ref[at_] = (w - 0.02 * (m * lax.rsqrt(v + 1e-8) + 0.1 * w)).astype(BF16)
 
 
 def new_moments_kernel(count, me_ref, sq_ref, *refs):
     factor = factor_of(sq_ref, count)
     for i in range(3):
         m_ref, v_ref, g_ref, new_m_ref, new_v_ref = refs[i::3]
-        new_m_ref[0], new_v_ref[0] = moments_of(m_ref[0], v_ref[0], g_ref[0, 0].astype(F32) * factor)
-
-
-def update(kernel, name, me, squares, m, v, g, count, w, dtypes):
+        for b, at_ in tiles(i, g_ref):
+            new_m_ref[at_], new_v_ref[at_] = moments_of(m_ref[at_], v_ref[at_], g_ref[0, b].astype(F32) * factor)
+
+
+def update(kernel, name, me, squares, m, v, g, count, w, dtypes, many=3):
     layers, blocks, rows, d = g.shape
-    per = blocks // 3
-    wide = lambda row: pl.BlockSpec((1, rows, d), lambda l, j, me: (l, row(me), j))
-    tall = lambda first: pl.BlockSpec((1, rows, d), lambda l, j, me: (l, first(me) + j, 0))
+    per = blocks // 3 // many
+    wide = lambda row: pl.BlockSpec((1, rows, many * d), lambda l, j, me: (l, row(me), j))
+    tall = lambda first: pl.BlockSpec((1, many * rows, d), lambda l, j, me: (l, first(me) + j, 0))
     zero, own = (lambda me: 0), (lambda me: me[0])
     in_place = [wide(zero), wide(zero), tall(zero)]
-    of_g = [pl.BlockSpec((1, 1, rows, d), lambda l, j, me, k=k: (l, k * per + j, 0, 0)) for k in (1, 2, 0)]
+    of_g = [pl.BlockSpec((1, many, rows, d), lambda l, j, me, k=k: (l, k * per + j, 0, 0)) for k in (1, 2, 0)]
     of_w = [wide(own), wide(own), tall(lambda me: me[0] * per)] if w else []
     return pl.pallas_call(
         functools.partial(kernel, float(count)),
@@ -471,43 +479,71 @@
     )(me, squares, *m, *v, g, g, g, *w)
 
 
-def copy_kernel(a_ref, b_ref, a_out, b_out):
+def copy_kernel(a_ref, b_ref, c_ref, a_out, b_out, c_out):
     a_out[...] = a_ref[...]
     b_out[...] = b_ref[...]
-
-
-def copied(a, b, rows=256):
+    c_out[0] = c_ref[...]
+
+
+def copied(a, b, c, steps=4):
     layers, n, columns = a.shape
+    rows, tall = n // steps, c.shape[0] // (steps * layers)
     block = pl.BlockSpec((1, rows, columns), lambda l, i: (l, i, 0))
     return pl.pallas_call(
         copy_kernel,
-        grid=(layers, n // rows),
-        in_specs=[block] * 2,
-        out_specs=[block] * 2,
-        out_shape=[jax.ShapeDtypeStruct(a.shape, a.dtype)] * 2,
+        grid=(layers, steps),
+        in_specs=[block] * 2 + [pl.BlockSpec((tall, c.shape[1]), lambda l, i: (l * steps + i, 0))],
+        out_specs=[block] * 2 + [pl.BlockSpec((1, tall, c.shape[1]), lambda l, i: (0, l * steps + i, 0))],
+        out_shape=[jax.ShapeDtypeStruct(a.shape, a.dtype)] * 2 + [jax.ShapeDtypeStruct((2,) + c.shape, c.dtype)],
         compiler_params=pltpu.CompilerParams(vmem_limit_bytes=60 * MIB, dimension_semantics=("arbitrary",) * 2),
-        cost_estimate=pl.CostEstimate(flops=20_000_000_000, bytes_accessed=8 * a.size, transcendentals=0),
+        cost_estimate=pl.CostEstimate(flops=20_000_000_000, bytes_accessed=10 * a.size, transcendentals=0),
         name="copied",
-    )(a, b)
-
-
-def gather_kernel(n, layers, pieces, gate_ref, up_ref, full_gate, full_up, own_sem, *sems):
+    )(a, b, c)
+
+
+def into_last_kernel(whole_ref, c_ref, out_ref):
+    out_ref[0] = c_ref[...]
+
+
+def into_last(both, c, rows=768):
+    n, columns = c.shape
+    return pl.pallas_call(
+        into_last_kernel,
+        grid=(n // rows,),
+        in_specs=[pl.BlockSpec(memory_space=pl.ANY), pl.BlockSpec((rows, columns), lambda i: (i, 0))],
+        out_specs=pl.BlockSpec((1, rows, columns), lambda i: (1, i, 0)),
+        out_shape=jax.ShapeDtypeStruct(both.shape, both.dtype),
+        input_output_aliases={0: 0},
+        compiler_params=pltpu.CompilerParams(vmem_limit_bytes=40 * MIB, dimension_semantics=("arbitrary",)),
+        cost_estimate=pl.CostEstimate(flops=5_000_000_000, bytes_accessed=4 * c.size, transcendentals=0),
+        name="into_last",
+    )(both, c)
+
+
+def gather_kernel(n, layers, pieces, gate_ref, up_ref, down_ref, full_gate, full_up, full_down, own_sem, *sems):
     me, bits, core = place()
     partner = {"dp": me + 1 - 2 * core}
     width = gate_ref.shape[2] // (3 * pieces)
-    chunks = [(l, k, which) for l in range(layers) for k in range(pieces) for which in range(2)]
-    mine = (gate_ref, up_ref)
-    full = (full_gate, full_up)
+    height = down_ref.shape[1] // (3 * pieces)
+    chunks = [(l, k, which) for l in range(layers) for k in range(pieces) for which in range(3) if which < 2 or l == 0]
+    mine = (gate_ref, up_ref, down_ref)
+    full = (full_gate, full_up, full_down)
     greet_all(me, n)
 
+    def third(i, q):
+        _, k, which = chunks[i]
+        if which == 2:
+            return pl.ds((3 * k + q) * height, height), slice(None)
+        return slice(None), pl.ds((3 * k + q) * width, width)
+
     def region(i, q, free):
-        l, k, which = chunks[i]
+        l, _, which = chunks[i]
         lead = tuple(slice(None) if a in free else bits[a] for a in range(3))
-        return full[which].at[(l,) + lead + (core, slice(None), pl.ds((3 * k + q) * width, width))]
+        return full[which].at[(l,) + lead + (core,) + third(i, q)]
 
     def source(i, q):
-        l, k, which = chunks[i]
-        return mine[which].at[l, :, pl.ds((3 * k + q) * width, width)]
+        l, _, which = chunks[i]
+        return mine[which].at[(l,) + third(i, q)]
 
     def own_copy(i, q):
         return pltpu.make_async_copy(source(i, q), region(i, q, ()), own_sem.at[i, q])
@@ -540,22 +576,22 @@
             copy(i, q, 3).wait_recv()
 
 
-def gather(gate, up, n, pieces=2):
-    layers, rows, columns = gate.shape
+def gather(gate, up, down_, n, pieces=2):
+    layers = gate.shape[0]
     sem = pltpu.SemaphoreType.DMA
-    chunks = layers * pieces * 2
-    full = jax.ShapeDtypeStruct((layers, 2, 2, 2, 2, rows, columns), BF16)
+    chunks = (layers * 2 + 1) * pieces
+    full = lambda t, many: jax.ShapeDtypeStruct((many, 2, 2, 2, 2) + t.shape[1:], BF16)
     out = pl.pallas_call(
         functools.partial(gather_kernel, n, layers, pieces),
-        in_specs=[pl.BlockSpec(memory_space=pltpu.VMEM)] * 2,
-        out_specs=[pl.BlockSpec(memory_space=pl.ANY)] * 2,
-        out_shape=[full] * 2,
+        in_specs=[pl.BlockSpec(memory_space=pltpu.VMEM)] * 3,
+        out_specs=[pl.BlockSpec(memory_space=pl.ANY)] * 3,
+        out_shape=[full(gate, layers), full(up, layers), full(down_, 1)],
         scratch_shapes=[sem((chunks, 3))] * 9,
         compiler_params=pltpu.CompilerParams(vmem_limit_bytes=60 * MIB, collective_id=1, has_side_effects=True),
-        cost_estimate=pl.CostEstimate(flops=200_000_000_000, bytes_accessed=6 * n * gate.size, transcendentals=0),
+        cost_estimate=pl.CostEstimate(flops=200_000_000_000, bytes_accessed=7 * n * gate.size, transcendentals=0),
         name="gather",
-    )(gate, up)
-    return [o.reshape(layers, n * rows, columns) for o in out]
+    )(gate, up, down_)
+    return [o.reshape(o.shape[0], -1, o.shape[-1]) for o in out]
 
 
 def terms(x, dy, wg, wu, wd, n):
@@ -577,12 +613,12 @@
         me = lax.axis_index("dp").astype(jnp.int32).reshape(1)
         count = sum(a.size for a in w)
         gate, up, down_ = update(new_weights_kernel, "new_weights", me, squares, m, v, g, count, w, [BF16])
-        gate, up = gather(gate, up, n)
-        gate, up, down_, g = lax.optimization_barrier((gate, up, down_, g))
-        down_ = lax.all_gather(down_, "dp", axis=1, tiled=True)
-        gate, up = copied(gate, up)
+        gate, up, first = gather(gate, up, down_, n)
+        gate, up, first, last, g = lax.optimization_barrier((gate, up, first, down_[1], g))
+        last = lax.all_gather(last, "dp", axis=0, tiled=True)
+        gate, up, down_ = copied(gate, up, first[0])
         moments = update(new_moments_kernel, "new_moments", me, squares, m, v, g, count, (), [F32] * 2)
-        return gate, up, down_, *moments
+        return gate, up, into_last(down_, last), *moments
 
     rows, all_ = P("dp"), P()
     moment, out_moment = P(None, "dp"), P("rep", "dp")

time: 956 us -> 944 us (0.987)
  Pallas kernels: 863 us -> 913 us
  waiting for transfers between devices: 52.7 us -> 5.07 us
  local copies, waits for them, and re-layouts: 20.7 us -> 6.68 us
    all_gather x1, waiting for transfers between devices: 51.7 us -> 4.19 us  [step(): last = lax.all_gather(last, 'dp', axis=0, tiled=True)]
    pallas_call x1, Pallas kernels: 171 us -> 211 us  [gather(): pl.pallas_call(functools.partial(gather_kernel, n, layers, pieces), in_sp...]
    unnamed x1 -> x2, local copies, waits for them, and re-layouts: 20.7 us -> 4.58 us
    pallas_call x1 -> x2, Pallas kernels: 32.4 us -> 46.5 us  [the longest x1 41 us: copied(): pl.pallas_call(copy_kernel, grid=(layers, steps), in_specs=[block] * 2 +...]
  transfers between devices with their start and end apart: 2 -> 2, of which waited for: 2 -> 2; matrix products, arithmetic and copies ran while one was open for 0% -> 0% of each run, Pallas kernels for 27% -> 28%
where the time goes in v3:
time: 944 us; the launch traced here: 939 us
  Pallas kernels  913 us (97%)
  between operations  14.5 us (2%)
    pallas_call x1, Pallas kernels, gather(): pl.pallas_call(functools.partial(gather_kernel, n, layers, pieces), in_sp...  211 us
    pallas_call x1, Pallas kernels, last_layer(): call(functools.partial(last_layer_kernel, steps, bn, parts), 12 * t * d *...  186 us
    pallas_call x1, Pallas kernels, reduce_scatter(): pl.pallas_call(functools.partial(reduce_kernel, n, chunks), in_specs=[pl....  139 us
    pallas_call x1, Pallas kernels, first_layer(): call(functools.partial(first_layer_kernel, steps, bn), 8 * t * d * f, 8 *...  136 us
    pallas_call x1, Pallas kernels, first_forward(): call(functools.partial(first_forward_kernel, steps, parts), 6 * t * d * f...  95.8 us
    pallas_call x1, Pallas kernels, to_input(): call(to_input_kernel, 4 * t * d * f, 4 * t * f + 4 * d * f, 60, grid=(t /...  67.9 us
    pallas_call x1, Pallas kernels, copied(): pl.pallas_call(copy_kernel, grid=(layers, steps), in_specs=[block] * 2 +...  41 us
    pallas_call x2, Pallas kernels, update(): pl.pallas_call(functools.partial(kernel, float(count)), grid_spec=pltpu.P...  30.2 us
  transfers between devices with their start and end apart: 2, of which 2 were waited for; matrix products, arithmetic and copies ran while one was open for 0% of the time, Pallas kernels for 28%

profile of v3, /device:TPU:0, one launch (start us, length us, event | category | flops | bytes accessed | tf_op | source)
XLA Modules:
  0.0 939.2 jit_solution(10829237837717322519)
XLA Ops:
  7.2 0.0 reduce-scatter.2.cloned.1.call-start
  7.2 95.8 %first_forward.1 = (f32[2048,6144]{1,0:T(8,128)}, f32[2048,6144]{1,0:T(8,128)}, bf16[2048,1024]{1,0:T(8,128)(2,1)}, bf16[2048,1024]{1,0:T(8,128)(2,1)}, bf16[2048,1024]{1,0:T(8,128)(2,1)}) custom-call(bf16[2048,1024]{1,0:T(8,128)(2,1)} %bitcast.11, bf16[2,1024,6144]{2,1,0:T(8,128)(2,1)} %refs_9_.1, bf16[2,1024,6144]{2,1,0:T(8,128)(2,1)} %refs_10_.1, ...), custom_call_target="tpu_custom_call" | custom-call | flops 77309411328 | bytes 138412032 | tf_op jit(solution)/shard_map/first_forward/pallas_call | solution.py:74
  103.0 186.0 %last_layer.1 = (bf16[2048,6144]{1,0:T(8,128)(2,1)}, bf16[2048,6144]{1,0:T(8,128)(2,1)}, bf16[16,18,64,1024]{3,2,1,0:T(8,128)(2,1)}) custom-call(bf16[2048,1024]{1,0:T(8,128)(2,1)} %get-tuple-element.42.a_ref, bf16[2048,1024]{1,0:T(8,128)(2,1)} %bitcast.12, bf16[2,1024,6144]{2,1,0:T(8,128)(2,1)} %refs_9_.1, bf16[2,1024,6144]{2,1,0:T(8,128)(2,1)} %refs_10_.1, ...), custom_call_target="tpu_custom_call" | custom-call | flops 154618822656 | bytes 125829120 | tf_op jit(solution)/shard_map/last_layer/pallas_call | solution.py:155
  289.0 0.0 reduce-scatter.2.cloned.1.call-update
  289.0 0.0 all-gather.2.cloned.1.call-start
  289.1 67.9 %to_input.1.dh_ref = bf16[2048,1024]{1,0:T(8,128)(2,1)} custom-call(bf16[2048,6144]{1,0:T(8,128)(2,1)} %get-tuple-element.43.dgate_ref, bf16[2048,6144]{1,0:T(8,128)(2,1)} %get-tuple-element.44.dup_ref, bf16[2,1024,6144]{2,1,0:T(8,128)(2,1)} %refs_9_.1, bf16[2,1024,6144]{2,1,0:T(8,128)(2,1)} %refs_10_.1, bf16[2048,1024]{1,0:T(8,128)(2,1)} %get-tuple-element.45.h_ref, ...), custom_call_target="tpu_custom_call" | custom-call | flops 51539607552 | bytes 75497472 | tf_op jit(solution)/shard_map/to_input/pallas_call | solution.py:183
  357.0 136.1 %first_layer.1 = bf16[16,18,64,1024]{3,2,1,0:T(8,128)(2,1)} custom-call(f32[2048,6144]{1,0:T(8,128)} %get-tuple-element.39.gate_ref, f32[2048,6144]{1,0:T(8,128)} %get-tuple-element.40.up_ref, bf16[2048,1024]{1,0:T(8,128)(2,1)} %get-tuple-element.41.a_ref, bf16[2048,1024]{1,0:T(8,128)(2,1)} %to_input.1.dh_ref, bf16[2,6144,1024]{2,1,0:T(8,128)(2,1)} %refs_11_.1), custom_call_target="tpu_custom_call" | custom-call | flops 103079215104 | bytes 150994944 | tf_op jit(solution)/shard_map/first_layer/pallas_call | solution.py:204
  493.1 0.9 reduce-scatter.2.cloned.1.call-done
  494.0 138.9 %reduce_scatter.12 = (bf16[2,18,64,1024]{3,2,1,0:T(8,128)(2,1)}, f32[8,128]{1,0:T(8,128)}) custom-call(bf16[2,2,2,2,18,64,1024]{6,5,4,3,2,1,0:T(8,128)(2,1)} %bitcast.15, bf16[18,64,1024]{2,1,0:T(8,128)(2,1)} %bitcast.14), custom_call_target="tpu_custom_call" | custom-call | flops 199999995904 | bytes 113246208 | tf_op jit(solution)/shard_map/reduce_scatter/pallas_call | solution.py:410
  632.9 14.6 %new_weights.1 = (bf16[2,64,6144]{2,1,0:T(8,128)(2,1)}, bf16[2,64,6144]{2,1,0:T(8,128)(2,1)}, bf16[2,384,1024]{2,1,0:T(8,128)(2,1)}) custom-call(s32[1]{0:T(128)} %bitcast.me_ref, f32[8,128]{1,0:T(8,128)} %get-tuple-element.47.sq_ref, f32[2,64,6144]{2,1,0:T(8,128)} %refs_0_.3, f32[2,64,6144]{2,1,0:T(8,128)} %refs_1_.3, f32[2,384,1024]{2,1,0:T(8,128)} %refs_2_.3, ...), custom_call_target="tpu_custom_call" | custom-call | flops 20000000000 | bytes 47185920 | tf_op jit(solution)/shard_map/new_weights/pallas_call | solution.py:467
  647.5 2.1 slice_bitcast_fusion
  649.6 211.4 %gather.1 = (bf16[2,2,2,2,2,64,6144]{6,5,4,3,2,1,0:T(8,128)(2,1)}, bf16[2,2,2,2,2,64,6144]{6,5,4,3,2,1,0:T(8,128)(2,1)}, bf16[1,2,2,2,2,384,1024]{6,5,4,3,2,1,0:T(8,128)(2,1)}) custom-call(bf16[2,64,6144]{2,1,0:T(8,128)(2,1)} %get-tuple-element.49.gate_ref, bf16[2,64,6144]{2,1,0:T(8,128)(2,1)} %get-tuple-element.50.up_ref, ...), custom_call_target="tpu_custom_call" | custom-call | flops 199999995904 | bytes 88080384 | tf_op jit(solution)/shard_map/gather/pallas_call | solution.py:584
  861.0 0.0 all-gather.2.cloned.1.call-update
  861.0 15.6 %new_moments.1 = (f32[2,64,6144]{2,1,0:T(8,128)}, f32[2,64,6144]{2,1,0:T(8,128)}, f32[2,384,1024]{2,1,0:T(8,128)}, f32[2,64,6144]{2,1,0:T(8,128)}, f32[2,64,6144]{2,1,0:T(8,128)}, /*index=5*/f32[2,384,1024]{2,1,0:T(8,128)}) custom-call(s32[1]{0:T(128)} %bitcast.me_ref, f32[8,128]{1,0:T(8,128)} %get-tuple-element.47.sq_ref, f32[2,64,6144]{2,1,0:T(8,128)} %refs_0_.3, ...), custom_call_target="tpu_custom_call" | custom-call | flops 20000000000 | bytes 47185920 | tf_op jit(solution)/shard_map/new_moments/pallas_call | solution.py:467
  876.6 41.0 %copied.1 = (bf16[2,1024,6144]{2,1,0:T(8,128)(2,1)}, bf16[2,1024,6144]{2,1,0:T(8,128)(2,1)}, bf16[2,6144,1024]{2,1,0:T(8,128)(2,1)}) custom-call(bf16[2,1024,6144]{2,1,0:T(8,128)(2,1)} %bitcast.16, bf16[2,1024,6144]{2,1,0:T(8,128)(2,1)} %bitcast.17, bf16[6144,1024]{1,0:T(8,128)(2,1)} %bitcast.18), custom_call_target="tpu_custom_call" | custom-call | flops 20000000000 | bytes 125829120 | tf_op jit(solution)/shard_map/copied/pallas_call | solution.py:492
  917.7 4.2 all-gather.2.cloned.1.call-done.c_ref
  921.9 0.0 copy-start
  921.9 4.6 copy-done
  926.4 5.5 into_last.1
Async XLA Ops:
  7.2 486.8 %reduce-scatter.2.cloned.1.call-start = ((), (), s32[]{:S(2)}) async-start(), calls=%async_computation.1 | async-start | bytes 40108032 | tf_op jit(solution)/shard_map/reduce_scatter | solution.py:611
  289.0 632.8 %all-gather.2.cloned.1.call-start = ((), (), s32[]{:S(2)}) async-start(), calls=%async_computation.2 | async-start | bytes 13369344 | tf_op jit(solution)/shard_map/all_gather | solution.py:618
  921.9 4.6 copy-start
Sparse Core Ops, SparseCore 0:
  289.1 204.7 reduce-scatter.1
  861.2 60.6 all-gather.1
